TPU v7x, 32 devices: a whole 2x2x4 slice. The times are simulated.
32 devices in a mesh: seq: 8 (over y, x, core), zero: 4 (over z).
Axes of the slice: x: 2, y: 2, z: 4, core: 2. Of those that a mesh axis runs over, the one named last changes fastest.
Arguments:
- hidden: bfloat16 [4, 1024, 1280], P('zero', 'seq'), may hold values from -6 to 6
- output_grad: bfloat16 [4, 1024, 2560], P('zero', 'seq'), may hold values from -6 to 6
- input_weight: bfloat16 [1280, 2856], P('zero'), may hold values from -0.15625 to 0.15625
- step_bias: float32 [40], replicated, may hold values from -7 to -2
- decay_log: float32 [40], replicated, may hold values from -4 to 1
- skip_gain: float32 [40], replicated, may hold values from 0.5 to 1.5
Outputs:
- hidden_grad: bfloat16 [4, 1024, 1280], P('zero', 'seq')
- weight_grad: float32 [1280, 2856], P(('seq', 'zero'))
- head_grads: float32 [3, 40], replicated
All inputs are finite; a program needn't handle non-finite values.
Results may differ from a plain program's by a relative error of at most 0.0049.
Values may be sent and summed in bfloat16 or wider, within the bound.
A program may use at most 192 MiB of HBM per device.

v0:
```python
import functools

import jax
import jax.numpy as jnp
from jax import lax
from jax.experimental import pallas as pl
from jax.experimental.pallas import tpu as pltpu
from jax.sharding import PartitionSpec as P

HEAD_DIM = 64
STATE = 128
MESH = pl.DeviceIdType.MESH
F32 = jnp.float32
BF16 = jnp.bfloat16


def up(size, unit):
    return -(-size // unit) * unit


def nn(a, b):
    return lax.dot_general(a, b, (((1,), (0,)), ((), ())), preferred_element_type=F32)


def nt(a, b):
    return lax.dot_general(a, b, (((1,), (1,)), ((), ())), preferred_element_type=F32)


def tn(a, b):
    return lax.dot_general(a, b, (((0,), (0,)), ((), ())), preferred_element_type=F32)


def halves(a):
    high = a.astype(BF16)
    return high, (a - high.astype(F32)).astype(BF16)


def fine(dot, a, b):
    if a.dtype == BF16:
        high, low = halves(b)
        return dot(a, high) + dot(a, low)
    if b.dtype == BF16:
        high, low = halves(a)
        return dot(high, b) + dot(low, b)
    (ah, al), (bh, bl) = halves(a), halves(b)
    return dot(ah, bh) + (dot(al, bh) + dot(ah, bl))


def exact(a, b):
    return lax.dot_general(
        a, b, (((1,), (0,)), ((), ())), precision=lax.Precision.HIGHEST, preferred_element_type=F32
    )


def greet(peers):
    barrier = pltpu.get_barrier_semaphore()
    for peer in peers:
        pl.semaphore_signal(barrier, inc=1, device_id=peer, device_id_type=MESH)
    pl.semaphore_wait(barrier, len(peers))


def remote(src, dst, send, recv, peer):
    return pltpu.make_async_remote_copy(src, dst, send, recv, peer, MESH)


def collect_kernel(
    seqs, zeros, tok, cot, wgt, tok_out, cot_out, wgt_out, wsib_out,
    tsem, fsem, csem, rsem, ssem, loc,
):
    me_s, me_z = lax.axis_index("seq"), lax.axis_index("zero")
    chips = seqs // 2
    chip, core = me_s // 2, lax.rem(me_s, 2)
    sibling = (chip * 2 + 1 - core, me_z)
    half = wgt.shape[0] // 2
    full_hops = (zeros - 1) // 2
    upper, lower = pl.ds(0, half), pl.ds(half, wgt.shape[0] - half)

    def along(step):
        return (lax.rem(me_s + step, seqs), me_z)

    def owner(shift):
        return lax.rem(me_z + shift + zeros, zeros)

    right, left = (me_s, owner(1)), (me_s, owner(-1))
    greet([along(i) for i in range(1, seqs)] + ([right, left] if zeros > 1 else []))

    own = [
        pltpu.make_async_copy(tok, tok_out.at[me_s], loc.at[0]),
        pltpu.make_async_copy(cot.at[me_s], cot_out.at[me_s], loc.at[1]),
        pltpu.make_async_copy(wgt, wgt_out.at[me_z], loc.at[2]),
    ]

    def hop(way, h):
        at = owner(-way * (h - 1))
        src = wgt if h == 1 else wgt_out.at[at]
        dst = wgt_out.at[at]
        if h > full_hops:
            rows = upper if way > 0 else lower
            src, dst = src.at[rows], dst.at[rows]
        row = 0 if way > 0 else 2
        return remote(src, dst, rsem.at[row, h], rsem.at[row + 1, h], right if way > 0 else left)

    hops = full_hops + (1 - zeros % 2)
    ring = [(hop(1, h), hop(-1, h)) for h in range(1, hops + 1)]

    def token_slot(step):
        return lax.rem(chip - step + chips, chips) * 2 + core

    tokens = [
        remote(
            tok, tok_out.at[me_s], tsem.at[0, d], tsem.at[1, d],
            (lax.rem(chip + d, chips) * 2 + core, me_z),
        )
        for d in range(1, chips)
    ]
    cots = []
    for d in range(1, seqs):
        peer = along(d)
        cots.append(
            remote(cot.at[peer[0]], cot_out.at[me_s], csem.at[0, d], csem.at[1, d], peer)
        )
    passed = [remote(tok, tok_out.at[me_s], fsem.at[0, 0], fsem.at[1, 0], sibling)]
    for d in range(1, chips):
        at = token_slot(d)
        passed.append(remote(tok_out.at[at], tok_out.at[at], fsem.at[0, d], fsem.at[1, d], sibling))

    def share(slot, at, src):
        return remote(src, wsib_out.at[at], ssem.at[0, slot], ssem.at[1, slot], sibling)

    shared = [share(0, me_z, wgt)]
    for d in range(1, zeros):
        at = owner(-d)
        shared.append(share(d, at, wgt_out.at[at]))

    for copy in ring[0] if ring else ():
        copy.start()
    for copy in tokens + cots + [passed[0], shared[0]] + own:
        copy.start()
    for h in range(1, hops):
        for way in (0, 1):
            ring[h - 1][way].wait_recv()
            ring[h][way].start()
    for d in range(1, chips):
        tokens[d - 1].wait_recv()
        passed[d].start()
    if ring:
        for way in (0, 1):
            ring[-1][way].wait_recv()
    for copy in shared[1:]:
        copy.start()
    for pair in ring:
        for copy in pair:
            copy.wait_send()
    for copy in tokens:
        copy.wait_send()
    for copy in own + cots + passed + shared:
        copy.wait()


def collect(tok, cot, wgt, seqs, zeros):
    anywhere = pl.BlockSpec(memory_space=pl.ANY)
    columns = jax.ShapeDtypeStruct((zeros,) + wgt.shape, wgt.dtype)
    return pl.pallas_call(
        functools.partial(collect_kernel, seqs, zeros),
        out_shape=(
            jax.ShapeDtypeStruct((seqs,) + tok.shape, tok.dtype),
            jax.ShapeDtypeStruct(cot.shape, cot.dtype),
            columns,
            columns,
        ),
        in_specs=[anywhere] * 3,
        out_specs=(anywhere,) * 4,
        scratch_shapes=[
            pltpu.SemaphoreType.DMA((2, seqs)),
            pltpu.SemaphoreType.DMA((2, seqs)),
            pltpu.SemaphoreType.DMA((2, seqs)),
            pltpu.SemaphoreType.DMA((4, zeros + 1)),
            pltpu.SemaphoreType.DMA((2, zeros)),
            pltpu.SemaphoreType.DMA((3,)),
        ],
        compiler_params=pltpu.CompilerParams(collective_id=0, has_side_effects=True),
        name="collect",
    )(tok, cot, wgt)


def swap_kernel(give, maps, got, got_map, send, recv):
    me_s, me_z = lax.axis_index("seq"), lax.axis_index("zero")
    core = lax.rem(me_s, 2)
    sibling = (me_s // 2 * 2 + 1 - core, me_z)
    greet([sibling])
    copies = [
        remote(maps.at[1 - core], got_map, send.at[0], recv.at[0], sibling),
        remote(give.at[1], got, send.at[1], recv.at[1], sibling),
    ]
    for copy in copies:
        copy.start()
    for copy in copies:
        copy.wait()


def swap(split, maps):
    anywhere = pl.BlockSpec(memory_space=pl.ANY)
    return pl.pallas_call(
        swap_kernel,
        out_shape=(
            jax.ShapeDtypeStruct(split.shape[1:], split.dtype),
            jax.ShapeDtypeStruct(maps.shape[1:], maps.dtype),
        ),
        in_specs=[anywhere, anywhere],
        out_specs=(anywhere, anywhere),
        scratch_shapes=[pltpu.SemaphoreType.DMA((2,)), pltpu.SemaphoreType.DMA((2,))],
        compiler_params=pltpu.CompilerParams(collective_id=2, has_side_effects=True),
        name="swap",
    )(split, maps)


def deliver_kernel(
    seqs, zeros, tok, wgt, head, tok_out, wgt_out, head_out,
    zin, zsum, hin, hsum, tsem, zsem, wsem, hsem, gsem, loc,
):
    me_s, me_z = lax.axis_index("seq"), lax.axis_index("zero")
    chips = seqs // 2
    chip, core = me_s // 2, lax.rem(me_s, 2)
    greet(
        [(me_s, lax.rem(me_z + d, zeros)) for d in range(1, zeros)]
        + [(lax.rem(me_s + d, seqs), me_z) for d in range(1, seqs)]
    )
    across = []
    for d in range(1, zeros):
        target = lax.rem(me_z + d, zeros)
        across.append(
            remote(wgt.at[:, target], zin.at[d], zsem.at[0, d], zsem.at[1, d], (me_s, target))
        )
        across.append(remote(head, hin.at[d], hsem.at[0, d], hsem.at[1, d], (me_s, target)))
    tokens = []
    for d in range(1, chips):
        target = lax.rem(chip + d, chips)
        tokens.append(
            remote(
                tok.at[target], tok_out.at[chip], tsem.at[0, d], tsem.at[1, d],
                (target * 2 + core, me_z),
            )
        )
    own = [pltpu.make_async_copy(tok.at[chip], tok_out.at[chip], loc.at[0])]
    first = [
        pltpu.make_async_copy(wgt.at[:, me_z], zin.at[0], loc.at[2]),
        pltpu.make_async_copy(head, hin.at[0], loc.at[1]),
    ]
    for copy in across + tokens + first + own:
        copy.start()
    for copy in first + across:
        copy.wait()
    sums = hin[0]
    for d in range(1, zeros):
        sums = sums + hin[d]
    hsum[...] = sums

    def add(j, carry):
        total = zin[0, j].astype(F32)
        for d in range(1, zeros):
            total = total + zin[d, j].astype(F32)
        zsum[j] = total.astype(BF16)
        return carry

    lax.fori_loop(0, seqs, add, 0)
    own += [
        pltpu.make_async_copy(zsum.at[me_s], wgt_out.at[me_s], loc.at[3]),
        pltpu.make_async_copy(hsum, head_out.at[me_s], loc.at[4]),
    ]
    for copy in own[1:]:
        copy.start()
    along = []
    for d in range(1, seqs):
        target = lax.rem(me_s + d, seqs)
        along.append(
            remote(
                zsum.at[target], wgt_out.at[me_s], wsem.at[0, d], wsem.at[1, d], (target, me_z)
            )
        )
        along.append(
            remote(hsum, head_out.at[me_s], gsem.at[0, d], gsem.at[1, d], (target, me_z))
        )
    for copy in along:
        copy.start()
    for copy in own + tokens + along:
        copy.wait()


def deliver(tok, wgt, head, seqs, zeros):
    anywhere = pl.BlockSpec(memory_space=pl.ANY)
    block = wgt.shape[2:]
    return pl.pallas_call(
        functools.partial(deliver_kernel, seqs, zeros),
        out_shape=(
            jax.ShapeDtypeStruct(tok.shape, tok.dtype),
            jax.ShapeDtypeStruct((seqs,) + block, wgt.dtype),
            jax.ShapeDtypeStruct((seqs,) + head.shape, head.dtype),
        ),
        in_specs=[anywhere] * 3,
        out_specs=(anywhere,) * 3,
        scratch_shapes=[
            pltpu.VMEM((zeros, seqs) + block, BF16),
            pltpu.VMEM((seqs,) + block, BF16),
            pltpu.VMEM((zeros,) + head.shape, F32),
            pltpu.VMEM(head.shape, F32),
            pltpu.SemaphoreType.DMA((2, seqs)),
            pltpu.SemaphoreType.DMA((2, zeros)),
            pltpu.SemaphoreType.DMA((2, seqs)),
            pltpu.SemaphoreType.DMA((2, zeros)),
            pltpu.SemaphoreType.DMA((2, seqs)),
            pltpu.SemaphoreType.DMA((5,)),
        ],
        compiler_params=pltpu.CompilerParams(collective_id=1, has_side_effects=True),
        name="deliver",
    )(tok, wgt, head)


def mixer_kernel(hp, pre_ref, other_ref, dy_ref, par_ref, g_ref, split_ref, maps_ref, head_ref, states, grad, acc):
    chunks, inner, group = dy_ref.shape
    top = inner + STATE
    slots = acc.shape[1]
    core = lax.rem(lax.axis_index("seq"), 2)
    bias = par_ref[0][:, :1]
    rate = -jnp.exp(par_ref[1][:, :1])
    gain = par_ref[2][:, :1]
    row = lax.broadcasted_iota(jnp.int32, (group, group), 0)
    col = lax.broadcasted_iota(jnp.int32, (group, group), 1)
    causal = col >= row
    before = causal.astype(F32)
    after = (col <= row).astype(F32)

    def spread(rows):
        return jnp.concatenate(
            [jnp.broadcast_to(rows[h : h + 1], (HEAD_DIM, rows.shape[1])) for h in range(hp)], axis=0
        )

    def gather_rows(full):
        parts = [
            jnp.sum(full[h * HEAD_DIM : (h + 1) * HEAD_DIM], axis=0, keepdims=True) for h in range(hp)
        ]
        if slots > hp:
            parts.append(jnp.zeros((slots - hp, full.shape[1]), F32))
        return jnp.concatenate(parts, axis=0)

    def load(k):
        at = pl.ds(pl.multiple_of(k * group, group), group)
        pre = pre_ref[:inner, at]
        sig = jax.nn.sigmoid(pre)
        here, there = pre_ref[inner:top, at], other_ref[:, at]
        maps = jnp.concatenate(
            [jnp.where(core == 0, here, there), jnp.where(core == 0, there, here)], axis=0
        )
        map_sig = jax.nn.sigmoid(maps)
        raw = pre_ref[top : top + slots, at] + bias
        step = jax.nn.softplus(raw)
        cum = exact(rate * step, before)
        return at, pre, sig, maps, map_sig, raw, step, cum

    grad[...] = jnp.zeros_like(grad)

    def forward(k, carry):
        at, pre, sig, maps, map_sig, raw, step, cum = load(k)
        last = cum[:, group - 1 :]
        x = pre * sig
        in_map = maps[:STATE] * map_sig[:STATE]
        tail = x * spread(step * jnp.exp(last - cum))
        held = grad[...]
        states[k] = held
        grad[...] = spread(jnp.exp(jnp.broadcast_to(last, (slots, STATE)))) * held + fine(nt, tail, in_map)
        return carry

    lax.fori_loop(0, chunks, forward, 0)
    grad[...] = jnp.zeros_like(grad)
    acc[...] = jnp.zeros_like(acc)

    def backward(i, carry):
        k = chunks - 1 - i
        at, pre, sig, maps, map_sig, raw, step, cum = load(k)
        last = cum[:, group - 1 :]
        x = pre * sig
        both = maps * map_sig
        in_map = both[:STATE]
        out_map = both[STATE:]
        dy16 = dy_ref[k]
        dy = dy16.astype(F32)
        u = x * spread(step)
        tail = spread(jnp.exp(last - cum))
        lead = spread(jnp.exp(cum))
        leave = spread(jnp.exp(jnp.broadcast_to(last, (slots, STATE))))
        held = states[k]
        g_out = grad[...]
        u_tail = u * tail
        dy_lead = dy * lead

        score = fine(tn, in_map, out_map)
        cum_col = jnp.concatenate([cum, jnp.zeros((group - slots, group), F32)], axis=0).T
        d_score = jnp.zeros((group, group), F32)
        ksum = jnp.zeros((group, group), F32)
        du_parts = []
        r_parts = []
        for h in range(hp):
            at_h = slice(h * HEAD_DIM, (h + 1) * HEAD_DIM)
            diff = cum[h : h + 1] - cum_col[:, h : h + 1]
            within = jnp.where(causal, jnp.exp(jnp.where(causal, diff, 0.0)), 0.0)
            mixing = score * within
            d_mix = fine(tn, u[at_h], dy16[at_h])
            du_parts.append(fine(nt, dy16[at_h], mixing))
            d_score = d_score + d_mix * within
            pair = d_mix * mixing
            r_parts.append(jnp.sum(pair, axis=0, keepdims=True))
            ksum = jnp.where(col == h, jnp.sum(pair, axis=1, keepdims=True), ksum)
        if slots > hp:
            r_parts.append(jnp.zeros((slots - hp, group), F32))
        from_tail = fine(nn, g_out, in_map) * tail
        tail_rows = gather_rows(u * from_tail)
        lead_rows = gather_rows(dy_lead * fine(nn, held, out_map))
        du = jnp.concatenate(du_parts, axis=0) + from_tail
        d_cum = jnp.concatenate(r_parts, axis=0) - ksum.T[:slots] + lead_rows - tail_rows
        cross = jnp.sum(gather_rows(held * g_out * leave) + tail_rows, axis=1, keepdims=True)
        d_log = exact(d_cum, after) + cross
        d_step = gather_rows(du * x) + rate * d_log
        d_raw = d_step * jax.nn.sigmoid(raw)

        d_out = fine(nn, in_map, d_score) + fine(tn, held, dy_lead)
        d_in = fine(nt, out_map, d_score) + fine(tn, g_out, u_tail)
        grad[...] = leave * g_out + fine(nt, dy_lead, out_map)

        slope = sig * (1.0 + pre * (1.0 - sig))
        map_slope = map_sig * (1.0 + maps * (1.0 - map_sig))
        rest = g_ref.shape[0] - top - slots
        d_in = d_in * map_slope[:STATE]
        d_out = d_out * map_slope[STATE:]
        rounded = jnp.concatenate(
            [
                (du * spread(step) + dy * gain_full) * slope,
                jnp.where(core == 0, d_in, d_out),
                d_raw,
                jnp.zeros((rest, group), F32),
            ],
            axis=0,
        ).astype(BF16)
        g_ref[:, at] = rounded
        split_ref[lax.rem(k + core, 2), k // 2] = rounded
        maps_ref[0, :, at] = d_in
        maps_ref[1, :, at] = d_out
        acc[0] += d_raw
        acc[1] += d_log * (rate * step)
        acc[2] += gather_rows(dy * x)
        return carry

    gain_full = spread(jnp.broadcast_to(gain, (slots, group)))
    lax.fori_loop(0, chunks, backward, 0)
    lane = lax.broadcasted_iota(jnp.int32, head_ref.shape, 1)
    total = jnp.zeros(head_ref.shape, F32)
    for i in range(3):
        total = jnp.where(lane == i, jnp.sum(acc[i], axis=1, keepdims=True), total)
    head_ref[...] = total


def mixer(pre, other, dy, par, hp):
    chunks, inner, group = dy.shape
    slots = par.shape[1]
    return pl.pallas_call(
        functools.partial(mixer_kernel, hp),
        out_shape=(
            jax.ShapeDtypeStruct(pre.shape, BF16),
            jax.ShapeDtypeStruct((2, chunks // 2, pre.shape[0], group), BF16),
            jax.ShapeDtypeStruct((2, STATE, pre.shape[1]), F32),
            jax.ShapeDtypeStruct((slots, 128), F32),
        ),
        in_specs=[pl.BlockSpec(memory_space=pltpu.VMEM)] * 4,
        out_specs=(pl.BlockSpec(memory_space=pltpu.VMEM),) * 4,
        scratch_shapes=[
            pltpu.VMEM((chunks, inner, STATE), F32),
            pltpu.VMEM((inner, STATE), F32),
            pltpu.VMEM((3, slots, group), F32),
        ],
        compiler_params=pltpu.CompilerParams(vmem_limit_bytes=48 * 1024 * 1024),
        name="mixer",
    )(pre, other, dy, par)


def body(seqs, zeros, hidden, output_grad, input_weight, step_bias, decay_log, skip_gain):
    heads = step_bias.shape[0]
    hp = up(heads, seqs) // seqs
    slots = up(hp, 8)
    inner, full = hp * HEAD_DIM, heads * HEAD_DIM
    spare = seqs * hp - heads
    width = up(inner + STATE + slots, 128)
    me = lax.axis_index("seq")
    core = lax.rem(me, 2)
    mine = inner + STATE
    length, model = hidden.shape[1:]

    def own(array, axis, size, extra):
        if extra:
            pads = [(0, 0)] * array.ndim
            pads[axis] = (0, extra)
            array = jnp.pad(array, pads)
        return lax.dynamic_slice_in_dim(array, me * size, size, axis)

    weight = jnp.concatenate(
        [
            own(input_weight[:, :full], 1, inner, spare * HEAD_DIM),
            lax.dynamic_slice_in_dim(input_weight[:, full : full + 2 * STATE], core * STATE, STATE, 1),
            own(input_weight[:, full + 2 * STATE :], 1, hp, spare),
            jnp.zeros((input_weight.shape[0], width - mine - hp), BF16),
        ],
        axis=1,
    )
    cot = jnp.pad(output_grad[0], ((0, 0), (0, spare * HEAD_DIM))).T.reshape(seqs, inner, length)
    par = jnp.stack([own(v, 0, hp, spare) for v in (step_bias, decay_log, skip_gain)])
    par = jnp.broadcast_to(jnp.pad(par, ((0, 0), (0, slots - hp)))[:, :, None], (3, slots, 128))

    tokens, dy, columns, beside = collect(hidden[0], cot, weight, seqs, zeros)
    tokens = tokens.reshape(seqs * length, model)
    columns = columns.reshape(model, width)
    beside = beside.reshape(model, width)
    pre = lax.dot_general(columns, tokens, (((0,), (1,)), ((), ())), preferred_element_type=F32)
    other_pre = lax.dot_general(
        beside[:, inner:mine], tokens, (((0,), (1,)), ((), ())), preferred_element_type=F32
    )
    grads, split, maps, sums = mixer(pre, other_pre, dy, par, hp)
    other, other_map = swap(split, maps)
    pair_map = lax.dynamic_index_in_dim(maps, core, 0, False) + other_map
    grads = jnp.concatenate([grads[:inner], pair_map.astype(BF16), grads[mine:]], axis=0)

    def back(part, w):
        return lax.dot_general(part, w, (((1,), (1,)), ((), ())), preferred_element_type=F32)

    def parity(m):
        m = m.reshape(STATE, seqs // 2, 2, length)
        return lax.dynamic_index_in_dim(m, core, 2, False).transpose(1, 0, 2)

    def filled(part, middle):
        return jnp.concatenate([part[:, :inner], middle.astype(BF16), part[:, mine:]], axis=1)

    first = filled(split[0], parity(pair_map))
    rest_map = lax.dynamic_index_in_dim(maps, 1 - core, 0, False)
    second = filled(other, other[:, inner:mine].astype(F32) + parity(rest_map))
    token_part = (back(first, columns) + back(second, beside)).astype(BF16)
    weight_part = lax.dot_general(
        tokens, grads, (((0,), (1,)), ((), ())), preferred_element_type=F32
    ).astype(BF16)
    every = seqs * zeros
    weight_part = weight_part.reshape(seqs, zeros, model // every, width)

    token_all, rows, sums_all = deliver(token_part, weight_part, sums, seqs, zeros)
    token_grad = jnp.sum(token_all.astype(F32), axis=0).astype(BF16)
    rows = rows.astype(F32)
    parts = rows.transpose(1, 0, 2)
    weight_grad = jnp.concatenate(
        [
            parts[:, :, :inner].reshape(-1, seqs * inner)[:, :full],
            jnp.sum(rows[0::2, :, inner:mine], axis=0),
            jnp.sum(rows[1::2, :, inner:mine], axis=0),
            parts[:, :, mine : mine + hp].reshape(-1, seqs * hp)[:, :heads],
        ],
        axis=1,
    )
    head_grads = sums_all[:, :hp, :3].transpose(2, 0, 1).reshape(3, seqs * hp)[:, :heads]
    return (token_grad[None], weight_grad, head_grads)


def solution(mesh):
    placed = (P("zero", "seq", None), P("zero", "seq", None), P("zero", None), P(), P(), P())
    return jax.shard_map(
        functools.partial(body, mesh.shape["seq"], mesh.shape["zero"]),
        mesh=mesh,
        in_specs=placed,
        out_specs=(P("zero", "seq", None), P(("seq", "zero"), None), P()),
        check_vma=False,
    )
```

profile of v0, /device:TPU:9, one launch (start us, length us, event | category | flops | bytes accessed | tf_op | source)
XLA Modules:
  0.0 120.6 jit_solution(6540767198719107355)
XLA Ops:
  0.7 1.0 slice.52
  1.7 0.9 slice.53
  2.8 0.1 constant_dynamic-slice_fusion.5
  3.0 0.9 maximum_maximum_fusion.wgt
  3.9 1.1 copy.14
  5.0 31.2 %collect.1 = (bf16[8,128,1280]{2,1,0:T(8,128)(2,1)}, bf16[8,320,128]{2,1,0:T(8,128)(2,1)}, bf16[4,320,512]{2,1,0:T(8,128)(2,1)}, bf16[4,320,512]{2,1,0:T(8,128)(2,1)}) custom-call(bf16[128,1280]{1,0:T(8,128)(2,1)} %bitcast.60, bf16[8,320,128]{2,1,0:T(8,128)(2,1)} %bitcast.51, bf16[320,512]{1,0:T(8,128)(2,1)} %maximum_maximum_fusion.wgt), custom_call_target="tpu_custom_call" | custom-call | tf_op jit(solution)/shard_map/collect/pallas_call | solution.py:163
  36.2 3.3 %fusion.17.other_ref = f32[128,1024]{1,0:T(8,128)S(1)} fusion(bf16[1024,1280]{1,0:T(8,128)(2,1)} %bitcast.48, bf16[1280,512]{1,0:T(8,128)(2,1)} %bitcast.52), kind=kOutput, calls=%fused_computation.22 | convolution fusion | flops 335544320 | bytes 3473408 | tf_op jit(solution)/shard_map/dot_general | solution.py:520
  39.5 4.3 %fusion.25.pre_ref = f32[512,1024]{1,0:T(8,128)} fusion(bf16[1280,512]{1,0:T(8,128)(2,1)} %bitcast.55, bf16[1024,1280]{1,0:T(8,128)(2,1)S(1)} %bitcast.49), kind=kOutput, calls=%fused_computation.49 | convolution fusion | flops 1342177280 | bytes 6029312 | tf_op jit(solution)/shard_map/dot_general | solution.py:519
  44.1 18.7 %mixer.1 = (bf16[512,1024]{1,0:T(8,128)(2,1)S(1)}, bf16[2,4,512,128]{3,2,1,0:T(8,128)(2,1)S(1)}, f32[2,128,1024]{2,1,0:T(8,128)S(1)}, f32[8,128]{1,0:T(8,128)S(1)}) custom-call(f32[512,1024]{1,0:T(8,128)} %fusion.25.pre_ref, f32[128,1024]{1,0:T(8,128)S(1)} %fusion.17.other_ref, bf16[8,320,128]{2,1,0:T(8,128)(2,1)S(1)} %copy-done.5, ...), custom_call_target="tpu_custom_call" | custom-call | tf_op jit(solution)/shard_map/mixer/pallas_call | solution.py:463
  62.8 1.0 copy-done.1
  63.8 1.0 copy-done.3
  64.7 0.6 copy-done.6
  65.3 3.0 %swap.1 = (bf16[4,512,128]{2,1,0:T(8,128)(2,1)}, f32[128,1024]{1,0:T(8,128)}) custom-call(bf16[2,4,512,128]{3,2,1,0:T(8,128)(2,1)} %copy-done.3, f32[2,128,1024]{2,1,0:T(8,128)} %copy-done.1), custom_call_target="tpu_custom_call" | custom-call | tf_op jit(solution)/shard_map/swap/pallas_call | solution.py:203
  68.4 1.3 %bitcast_add_fusion = bf16[128,1024]{1,0:T(8,128)(2,1)S(1)} fusion(f32[128,1024]{1,0:T(8,128)} %get-tuple-element.22, f32[2,128,1024]{2,1,0:T(8,128)S(1)} %copy-done.2, s32[]{:T(128)S(6)} %select_n.25), kind=kLoop, calls=%fused_computation.19 | loop fusion | flops 262144 | bytes 1310724 | tf_op jit(solution)/shard_map/add | solution.py:525
  69.7 0.5 copy-done.8
  70.3 2.7 %convolution_convert_fusion = bf16[1280,512]{1,0:T(8,128)(2,1)} fusion(bf16[1024,1280]{1,0:T(8,128)(2,1)S(1)} %bitcast.50, bf16[64,1024]{1,0:T(8,128)(2,1)S(1)} %slice.62, bf16[128,1024]{1,0:T(8,128)(2,1)S(1)} %bitcast_add_fusion, bf16[320,1024]{1,0:T(8,128)(2,1)S(1)} %slice.61), kind=kOutput, calls=%fused_computation.1 | convolution fusion | flops 1345978368 | bytes 4980736 | tf_op jit(solution)/shard_map/dot_general | solution.py:542
  73.0 0.2 copy.17
  73.3 0.1 copy.18
  73.4 1.1 fusion.19
  74.5 0.2 reshape.43
  74.7 0.3 constant_dynamic-slice_fusion.2
  75.1 0.9 fusion.6
  76.0 0.1 copy-done.13
  76.2 0.4 copy-done.9
  76.6 2.0 %fusion.tok = bf16[4,128,1280]{2,1,0:T(8,128)(2,1)} fusion(f32[4,128,1280]{2,1,0:T(8,128)S(1)} %fusion.6, bf16[1280,512,1]{1,0,2:T(8,128)(2,1)S(1)} %bitcast.53, bf16[4,64,128]{2,1,0:T(8,128)(2,1)S(1)} %slice.60, bf16[4,128,128]{2,1,0:T(8,128)(2,1)S(1)} %fusion.19, bf16[4,320,128]{2,1,0:T(8,128)(2,1)S(1)} %slice.58), kind=kOutput, calls=%fused_computation.2 | convolution fusion | flops 673972224 | bytes 5767168 | tf_op jit(solution)/shard_map/dot_general | solution.py:529
  78.6 37.6 %deliver.1 = (bf16[4,128,1280]{2,1,0:T(8,128)(2,1)}, bf16[8,40,512]{2,1,0:T(8,128)(2,1)}, f32[8,8,128]{2,1,0:T(8,128)}) custom-call(bf16[4,128,1280]{2,1,0:T(8,128)(2,1)} %fusion.tok, bf16[8,4,40,512]{3,2,1,0:T(8,128)(2,1)} %bitcast.54, f32[8,128]{1,0:T(8,128)} %copy-done.6), custom_call_target="tpu_custom_call" | custom-call | tf_op jit(solution)/shard_map/deliver/pallas_call | solution.py:292
  116.2 1.1 fusion.24
  117.4 0.1 reshape.46
  118.0 0.8 pad_maximum_fusion
  118.8 1.0 reduce_sum.30
  119.8 0.1 copy.23
  120.0 0.7 reshape.48
  (56 shorter events, 1.3 us)
Async XLA Ops:
  0.6 43.3 %copy-start = (f32[40]{0:T(128)S(1)}, f32[40]{0:T(128)}, u32[]{:S(2)}) copy-start(f32[40]{0:T(128)} %param.9) | copy-start | bytes 484
  0.6 2.1 %slice-start = ((bf16[320,2856]{1,0:T(8,128)(2,1)}), bf16[320,2560]{1,0:T(8,128)(2,1)S(1)}, s32[]{:S(2)}) async-start(bf16[320,2856]{1,0:T(8,128)(2,1)} %param.8), calls=%async_computation | async-start | bytes 3276800 | tf_op jit(solution)/shard_map/slice | solution.py:504
  2.7 1.1 copy-start.12
  36.2 3.3 %copy-start.7 = (bf16[8,128,1280]{2,1,0:T(8,128)(2,1)S(1)}, bf16[8,128,1280]{2,1,0:T(8,128)(2,1)}, u32[]{:S(2)}) copy-start(bf16[8,128,1280]{2,1,0:T(8,128)(2,1)} %get-tuple-element.17) | copy-start | bytes 7864324
  39.5 4.3 %copy-start.15 = (f32[40]{0:T(128)S(1)}, f32[40]{0:T(128)}, u32[]{:S(2)}) copy-start(f32[40]{0:T(128)} %param.11) | copy-start | bytes 484
  39.5 4.3 %copy-start.16 = (f32[40]{0:T(128)S(1)}, f32[40]{0:T(128)}, u32[]{:S(2)}) copy-start(f32[40]{0:T(128)} %param.10) | copy-start | bytes 484
  39.5 4.5 %copy-start.5 = (bf16[8,320,128]{2,1,0:T(8,128)(2,1)S(1)}, bf16[8,320,128]{2,1,0:T(8,128)(2,1)}, u32[]{:S(2)}) copy-start(bf16[8,320,128]{2,1,0:T(8,128)(2,1)} %get-tuple-element.19.dy_ref) | copy-start | bytes 1966084
  62.8 1.0 copy-start.1
  63.8 1.0 copy-start.3
  64.7 0.6 copy-start.6
  65.3 3.1 %copy-start.2 = (f32[2,128,1024]{2,1,0:T(8,128)S(1)}, f32[2,128,1024]{2,1,0:T(8,128)}, u32[]{:S(2)}) copy-start(f32[2,128,1024]{2,1,0:T(8,128)} %copy-done.1) | copy-start | bytes 3145732
  68.4 1.9 %copy-start.8 = (bf16[8,128,1280]{2,1,0:T(8,128)(2,1)S(1)}, bf16[8,128,1280]{2,1,0:T(8,128)(2,1)}, u32[]{:S(2)}) copy-start(bf16[8,128,1280]{2,1,0:T(8,128)(2,1)} %get-tuple-element.17) | copy-start | bytes 7864324
  73.0 2.0 %copy-start.4 = (bf16[2,4,512,128]{3,2,1,0:T(8,128)(2,1)S(1)}, bf16[2,4,512,128]{3,2,1,0:T(8,128)(2,1)}, u32[]{:S(2)}) copy-start(bf16[2,4,512,128]{3,2,1,0:T(8,128)(2,1)} %copy-done.3) | copy-start | bytes 3145732
  73.3 1.8 %copy-start.11 = (bf16[4,320,512]{2,1,0:T(8,128)(2,1)S(1)}, bf16[4,320,512]{2,1,0:T(8,128)(2,1)}, u32[]{:S(2)}) copy-start(bf16[4,320,512]{2,1,0:T(8,128)(2,1)} %get-tuple-element.16) | copy-start | bytes 3932164
  75.1 1.0 copy-start.13
  75.1 1.5 %copy-start.9 = (bf16[4,320,512]{2,1,0:T(8,128)(2,1)S(1)}, bf16[4,320,512]{2,1,0:T(8,128)(2,1)}, u32[]{:S(2)}) copy-start(bf16[4,320,512]{2,1,0:T(8,128)(2,1)} %get-tuple-element.18) | copy-start | bytes 3932164
  117.3 1.6 %copy-start.10 = (bf16[4,128,1280]{2,1,0:T(8,128)(2,1)S(1)}, bf16[4,128,1280]{2,1,0:T(8,128)(2,1)}, u32[]{:S(2)}) copy-start(bf16[4,128,1280]{2,1,0:T(8,128)(2,1)} %get-tuple-element.26) | copy-start | bytes 3932164
  117.6 2.3 %copy-start.14 = (f32[8,8,128]{2,1,0:T(8,128)S(1)}, f32[8,8,128]{2,1,0:T(8,128)}, u32[]{:S(2)}) copy-start(f32[8,8,128]{2,1,0:T(8,128)} %get-tuple-element.28) | copy-start | bytes 98308
where the time goes:
time: 121 us
  Pallas kernels  90.5 us (75%)
  matrix products  13.1 us (11%)
  local copies, waits for them, and re-layouts  9.65 us (8%)
  other arithmetic  6.28 us (5%)
    pallas_call x1, Pallas kernels, deliver(): pl.pallas_call(functools.partial(deliver_kernel, seqs, zeros), out_shape=...  37.6 us
    pallas_call x1, Pallas kernels, collect(): pl.pallas_call(functools.partial(collect_kernel, seqs, zeros), out_shape=...  31.2 us
    pallas_call x1, Pallas kernels, mixer(): pl.pallas_call(functools.partial(mixer_kernel, hp), out_shape=(jax.ShapeD...  18.7 us
    dot_general x1, matrix products, body(): lax.dot_general(columns, tokens, (((0,), (1,)), ((), ())), preferred_elem...  4.29 us
    unnamed x35, local copies, waits for them, and re-layouts  3.7 us
    dot_general x1, matrix products, body(): lax.dot_general(beside[:, inner:mine], tokens, (((0,), (1,)), ((), ())),...  3.3 us
    pallas_call x1, Pallas kernels, swap(): pl.pallas_call(swap_kernel, out_shape=(jax.ShapeDtypeStruct(split.shape[1...  3.04 us
    dot_general x2, matrix products, back(): lax.dot_general(part, w, (((1,), (1,)), ((), ())), preferred_element_type...  2.88 us

commit v1 on v0

v1 whole, which is shorter than its diff:
```python
import functools

import jax
import jax.numpy as jnp
from jax import lax
from jax.experimental import pallas as pl
from jax.experimental.pallas import tpu as pltpu
from jax.sharding import PartitionSpec as P

HEAD_DIM = 64
STATE = 128
MESH = pl.DeviceIdType.MESH
F32 = jnp.float32
BF16 = jnp.bfloat16


def up(size, unit):
    return -(-size // unit) * unit


def nn(a, b):
    return lax.dot_general(a, b, (((1,), (0,)), ((), ())), preferred_element_type=F32)


def nt(a, b):
    return lax.dot_general(a, b, (((1,), (1,)), ((), ())), preferred_element_type=F32)


def tn(a, b):
    return lax.dot_general(a, b, (((0,), (0,)), ((), ())), preferred_element_type=F32)


def halves(a):
    high = a.astype(BF16)
    return high, (a - high.astype(F32)).astype(BF16)


def greet(peers):
    barrier = pltpu.get_barrier_semaphore()
    for peer in peers:
        pl.semaphore_signal(barrier, inc=1, device_id=peer, device_id_type=MESH)
    pl.semaphore_wait(barrier, len(peers))


def remote(src, dst, send, recv, peer):
    return pltpu.make_async_remote_copy(src, dst, send, recv, peer, MESH)


def mixer_backward_kernel(
    seqs, zeros, hp,
    hidden, cotangent, weight, bias_in, log_in, gain_in,
    hid, rows_out, head_out,
    window, tiny, cotv, cott,
    toks, tokt, wall, wallt, pre, dys, xs, tails, states, grads, grad, acc, steps, cums, cumt, sigr,
    maps, got_map, part, got_part, sent, tok_in, wbuf, rflow, lflow, zsend, rows_in, hin, hsum, hmine, hall,
    asem, tsem, psem, csem, ssem, msem, dsem, ksem, rsem, gsem, hsem, wsem, loc,
):
    me_s, me_z = lax.axis_index("seq"), lax.axis_index("zero")
    chips = seqs // 2
    chip, core = me_s // 2, lax.rem(me_s, 2)
    sib = me_s // 2 * 2 + 1 - core
    sibling = (sib, me_z)
    length, model = hidden.shape
    rows = weight.shape[0]
    width = wall.shape[1] - STATE
    inner = dys.shape[1]
    slots = acc.shape[1]
    full = cotangent.shape[1]
    chunks, group = seqs, length
    vals, top = STATE, STATE + inner
    up_peer, down_peer = (me_s, me_z + 1), (me_s, me_z - 1)
    half = rows // 2
    last_z = zeros - 1
    pairs = 2 * group

    start = pl.multiple_of(me_s * inner // 128 * 128, 128)
    mine = pl.ds(pl.multiple_of(me_z * rows, rows), rows)
    fetch = [
        pltpu.make_async_copy(weight.at[:, pl.ds(start, window.shape[1])], window, loc.at[0]),
        pltpu.make_async_copy(
            weight.at[:, pl.ds(pl.multiple_of(full + core * STATE, 128), STATE)],
            wall.at[mine, pl.ds(0, STATE)], loc.at[1],
        ),
        pltpu.make_async_copy(weight.at[:, pl.ds(full + 2 * STATE, tiny.shape[1])], tiny, loc.at[2]),
        pltpu.make_async_copy(hidden, toks.at[me_s], loc.at[3]),
        pltpu.make_async_copy(cotangent, cotv, loc.at[4]),
    ]
    for copy in fetch:
        copy.start()
    heads = tiny.shape[1]
    head_row = lax.broadcasted_iota(jnp.int32, (heads, width - top), 0)
    head_col = lax.broadcasted_iota(jnp.int32, (heads, width - top), 1)
    chosen = jnp.logical_and(head_row == me_s * hp + head_col, head_col < hp)
    chosen = jnp.where(chosen, 1.0, 0.0).astype(BF16)
    fetch[2].wait()
    wall[mine, top:width] = nn(tiny[...], chosen).astype(BF16)
    fetch[0].wait()
    if hp % 2:
        shifted = lax.rem(me_s, 2)
        for shift in (0, 1):
            @pl.when(shifted == shift)
            def _():
                wall[mine, vals:top] = window[:, shift * HEAD_DIM : shift * HEAD_DIM + inner]
    else:
        wall[mine, vals:top] = window[...]
    fetch[1].wait()
    fetch[3].wait()

    greet(
        [(lax.rem(me_s + d, seqs), me_z) for d in range(1, seqs)]
        + [(me_s, lax.rem(me_z + d, zeros)) for d in range(1, zeros)]
    )

    def piece(at, p):
        first = pl.multiple_of(at * rows + p * half, half)
        return wall.at[pl.ds(first, half), pl.ds(0, width)]

    def flow(way, h, p, recv):
        at = me_z - h if way == 0 else me_z + h
        return remote(
            piece(at, p), piece(at, p), asem.at[way, 0, h, p], asem.at[way, 1, h + (1 - recv), p],
            up_peer if way == 0 else down_peer,
        )

    def sends(way, h):
        if way == 0:
            return jnp.logical_and(me_z < last_z, me_z >= h)
        return jnp.logical_and(me_z > 0, me_z + h <= last_z)

    def comes(way, h):
        return me_z >= h if way == 0 else me_z + h <= last_z

    def shared(at):
        first = pl.multiple_of(at * rows, rows)
        return remote(
            wall.at[pl.ds(first, rows), pl.ds(0, STATE)],
            wall.at[pl.ds(first, rows), pl.ds(width, STATE)],
            ssem.at[0, at], ssem.at[1, at], sibling,
        )

    for p in (0, 1):
        for way in (0, 1):
            @pl.when(sends(way, 0))
            def _():
                flow(way, 0, p, 0).start()

    def token(src_s, dst, lo, size, slot):
        block = toks.at[src_s, pl.ds(lo, size)]
        return remote(block, block, tsem.at[0, slot], tsem.at[1, slot], (dst, me_z))

    def passed(src_s, slot):
        return remote(toks.at[src_s], toks.at[src_s], psem.at[0, slot], psem.at[1, slot], sibling)

    square = chips == 4
    cut = length // 2
    to_sibling = [passed(me_s, 0)]
    if square:
        flat = chip + 1 - 2 * lax.rem(chip, 2)
        tall = lax.rem(chip + 2, 4)
        far = lax.rem(flat + 2, 4)
        around = [flat, tall]
    else:
        around = [lax.rem(chip + d, chips) for d in range(1, chips)]
    direct = [token(me_s, c * 2 + core, 0, length, i) for i, c in enumerate(around)]
    for copy in direct + to_sibling:
        copy.start()
    shared(me_z).start()

    pre[...] = jnp.zeros_like(pre)
    fetch[4].wait()
    strip = 512

    def turn_cot(j, carry):
        at = pl.ds(pl.multiple_of(j * strip, strip), strip)
        cott[at, :] = cotv[:, at].T
        return carry

    lax.fori_loop(0, full // strip, turn_cot, 0)

    def cot_of(s):
        return cott.at[pl.ds(pl.multiple_of(s * inner, inner), inner)]

    dys[me_s] = cot_of(me_s)[...]

    def step_hop(h):
        for p in (0, 1):
            for way in (0, 1):
                @pl.when(comes(way, h))
                def _():
                    flow(way, h, p, 1).wait_recv()
                if h < last_z:
                    @pl.when(sends(way, h))
                    def _():
                        flow(way, h, p, 0).start()
        for way in (0, 1):
            @pl.when(comes(way, h))
            def _():
                shared(me_z - h if way == 0 else me_z + h).start()

    if zeros > 2:
        step_hop(1)

    if square:
        onward = [
            token(flat * 2 + core, tall * 2 + core, 0, cut, 2),
            token(tall * 2 + core, flat * 2 + core, cut, length - cut, 3),
        ]
        for i in (0, 1):
            direct[i].wait_recv()
            onward[i].start()
        direct += onward
        more = [passed(flat * 2 + core, 1), passed(tall * 2 + core, 2)]
    else:
        more = []
        for d in range(1, chips):
            direct[d - 1].wait_recv()
            more.append(passed(lax.rem(chip - d + chips, chips) * 2 + core, d))
    for copy in more:
        copy.start()
    to_sibling += more

    cots = []
    for d in range(1, seqs):
        peer = lax.rem(me_s + d, seqs)
        cots.append(remote(cot_of(peer), dys.at[me_s], csem.at[0, d], csem.at[1, d], (peer, me_z)))
    for copy in cots:
        copy.start()

    for h in range(2, last_z):
        step_hop(h)

    if square:
        token(far * 2 + core, tall * 2 + core, 0, cut, 2).wait_recv()
        token(far * 2 + core, flat * 2 + core, cut, length - cut, 3).wait_recv()
        to_sibling.append(passed(far * 2 + core, 3))
        to_sibling[-1].start()
    for copy in to_sibling:
        copy.wait_recv()

    def turn(k, carry):
        at = pl.ds(pl.multiple_of(k * group, group), group)
        tokt[:, at] = toks[k].T
        return carry

    lax.fori_loop(0, chunks, turn, 0)

    def project(j):
        shared(j).wait_recv()
        at = pl.ds(pl.multiple_of(j * rows, rows), rows)
        wallt[j] = wall[at, :].T

        def part_of(i, carry):
            cols = pl.ds(pl.multiple_of(i * pairs, pairs), pairs)
            pre[:, cols] += nn(wallt[j], tokt[at, cols])
            return carry

        lax.fori_loop(0, chunks // 2, part_of, 0)

    def near(j, carry):
        distance = jnp.abs(j - me_z)
        ready = distance < last_z if zeros > 1 else distance < 1

        @pl.when(ready)
        def _():
            project(j)
        return carry

    lax.fori_loop(0, zeros, near, 0)
    if zeros > 1:
        step_hop(last_z)
        far_end = jnp.logical_or(me_z == 0, me_z == last_z)

        @pl.when(far_end)
        def _():
            project(last_z - me_z)

    in_at = pl.multiple_of(core * width, 128)
    out_at = pl.multiple_of((1 - core) * width, 128)
    slot = lax.broadcasted_iota(jnp.int32, (slots, heads), 0)
    own_head = jnp.logical_and(
        lax.broadcasted_iota(jnp.int32, (slots, heads), 1) == me_s * hp + slot, slot < hp
    )

    def own(ref):
        return jnp.sum(jnp.where(own_head, ref[...], 0.0), axis=1, keepdims=True)

    bias, rate, gain = own(bias_in), -jnp.exp(own(log_in)), own(gain_in)
    row = lax.broadcasted_iota(jnp.int32, (group, group), 0)
    col = lax.broadcasted_iota(jnp.int32, (group, group), 1)
    causal = col >= row

    def spread(values):
        return jnp.concatenate(
            [jnp.broadcast_to(values[h : h + 1], (HEAD_DIM, values.shape[1])) for h in range(hp)], axis=0
        )

    def gather_rows(whole):
        parts = [
            jnp.sum(whole[h * HEAD_DIM : (h + 1) * HEAD_DIM], axis=0, keepdims=True) for h in range(hp)
        ]
        if slots > hp:
            parts.append(jnp.zeros((slots - hp, whole.shape[1]), F32))
        return jnp.concatenate(parts, axis=0)

    raw = pre[top : top + slots, :] + bias
    soft = jax.nn.softplus(raw)
    curve = jax.nn.sigmoid(raw)
    stacked = jnp.concatenate([soft[:, k * group : (k + 1) * group] for k in range(chunks)], axis=0)
    steps[...] = stacked
    sigr[...] = jnp.concatenate([curve[:, k * group : (k + 1) * group] for k in range(chunks)], axis=0)
    logs = jnp.concatenate([rate] * chunks, axis=0) * stacked
    before = jnp.where(causal, 1.0, 0.0).astype(BF16)
    after = jnp.where(col <= row, 1.0, 0.0).astype(BF16)

    def summed(values, mask):
        a = values.astype(BF16)
        rest = values - a.astype(F32)
        b = rest.astype(BF16)
        c = (rest - b.astype(F32)).astype(BF16)
        return nn(a, mask) + (nn(b, mask) + nn(c, mask))

    cums[...] = summed(logs, before)

    grad[...] = jnp.zeros_like(grad)

    def small(ref, k):
        return ref[pl.ds(pl.multiple_of(k * slots, slots), slots), :]

    def forward(k, carry):
        at = pl.ds(pl.multiple_of(k * group, group), group)
        p = pre[vals:top, at]
        sig = jax.nn.sigmoid(p)
        x = p * sig
        xs[k] = x
        pre[vals:top, at] = sig * (1.0 + p * (1.0 - sig))
        step, cum = small(steps, k), small(cums, k)
        last = cum[:, group - 1 :]
        m_in = pre[pl.ds(in_at, STATE), at]
        in16 = (m_in * jax.nn.sigmoid(m_in)).astype(BF16)
        tail16 = (x * spread(step * jnp.exp(last - cum))).astype(BF16)
        tails[k] = tail16
        cumt[k] = jnp.concatenate([cum, jnp.zeros((group - slots, group), F32)], axis=0).T
        held = grad[...]
        states[k] = held.astype(BF16)
        grad[...] = spread(jnp.exp(jnp.broadcast_to(last, (slots, STATE)))) * held + nt(tail16, in16)
        return carry

    lax.fori_loop(0, chunks, forward, 0)
    states[chunks] = grad[...].astype(BF16)
    grad[...] = jnp.zeros_like(grad)
    acc[...] = jnp.zeros_like(acc)
    gain_full = spread(jnp.broadcast_to(gain, (slots, group)))
    grads[pl.ds(top, width - top), :] = jnp.zeros((width - top, chunks * group), BF16)
    for copy in cots:
        copy.wait_recv()

    def map_copy(k):
        return remote(maps.at[1 - core, k], got_map.at[k], msem.at[0, k], msem.at[1, k], sibling)

    def backward(n, carry):
        k = chunks - 1 - n
        at = pl.ds(pl.multiple_of(k * group, group), group)
        step, cum = small(steps, k), small(cums, k)
        last = cum[:, group - 1 :]
        x = xs[k]
        step_full = spread(step)
        u16 = (x * step_full).astype(BF16)
        tail16 = tails[k]
        m_in, m_out = pre[pl.ds(in_at, STATE), at], pre[pl.ds(out_at, STATE), at]
        s_in, s_out = jax.nn.sigmoid(m_in), jax.nn.sigmoid(m_out)
        in16, out16 = (m_in * s_in).astype(BF16), (m_out * s_out).astype(BF16)
        dy16 = dys[k]
        dy = dy16.astype(F32)
        tail = spread(jnp.exp(last - cum))
        lead = spread(jnp.exp(cum))
        leave = spread(jnp.exp(jnp.broadcast_to(last, (slots, STATE))))
        held16 = states[k]
        g_out = grad[...]
        g16 = g_out.astype(BF16)
        dy_lead = dy * lead
        lead16 = dy_lead.astype(BF16)

        score = tn(in16, out16)
        cum_col = cumt[k]
        d_score = jnp.zeros((group, group), F32)
        du_parts, r_parts = [], []
        for h in range(hp):
            at_h = slice(h * HEAD_DIM, (h + 1) * HEAD_DIM)
            diff = cum[h : h + 1] - cum_col[:, h : h + 1]
            within = jnp.exp(jnp.where(causal, diff, -1e30))
            mixing = (score * within).astype(BF16)
            d_mix = tn(u16[at_h], dy16[at_h])
            du_parts.append(nt(dy16[at_h], mixing))
            d_score = d_score + d_mix * within
            r_parts.append(jnp.sum(d_mix * mixing.astype(F32), axis=0, keepdims=True))
        if slots > hp:
            r_parts.append(jnp.zeros((slots - hp, group), F32))
        du = jnp.concatenate(du_parts, axis=0) + nn(g16, in16) * tail
        from_x = gather_rows(du * x)
        from_u = gather_rows(du * u16.astype(F32))
        lead_rows = gather_rows(dy_lead * nn(held16, out16))
        cross = jnp.sum(gather_rows(g_out * states[k + 1].astype(F32)), axis=1, keepdims=True)
        d_cum = jnp.concatenate(r_parts, axis=0) + lead_rows - from_u
        d_log = summed(d_cum, after) + cross
        d_raw = (from_x + rate * d_log) * small(sigr, k)

        d_score16 = d_score.astype(BF16)
        d_out = nn(in16, d_score16) + tn(held16, lead16)
        d_in = nt(out16, d_score16) + tn(g16, tail16)
        grad[...] = leave * g_out + nt(lead16, out16)

        d_in = d_in * (s_in * (1.0 + m_in * (1.0 - s_in)))
        d_out = d_out * (s_out * (1.0 + m_out * (1.0 - s_out)))
        grads[vals:top, at] = ((du * step_full + dy * gain_full) * pre[vals:top, at]).astype(BF16)
        grads[pl.ds(in_at, STATE), at] = d_in.astype(BF16)
        grads[pl.ds(out_at, STATE), at] = d_out.astype(BF16)
        fill = jnp.zeros((16 - slots, group), F32)
        grads[top : top + 16, at] = jnp.concatenate([d_raw, fill], axis=0).astype(BF16)
        maps[0, k] = d_in
        maps[1, k] = d_out
        acc[0] += d_raw
        acc[1] += d_log * (rate * step)
        acc[2] += gather_rows(dy * x)
        map_copy(k).start()
        return carry

    lax.fori_loop(0, chunks, backward, 0)

    block = wbuf.shape[3]
    many = 4 if seqs % 4 == 0 else 2
    span = many * zeros * block

    def merge(k, carry):
        map_copy(k).wait_recv()
        at = pl.ds(pl.multiple_of(k * group, group), group)
        got_map[k] = maps[core, k] + got_map[k]
        return carry

    lax.fori_loop(0, chunks, merge, 0)
    own_map = jnp.concatenate([got_map[k].astype(BF16) for k in range(chunks)], axis=1)

    def weigh(q, carry):
        at = pl.ds(pl.multiple_of(q * span, span), span)
        product = jnp.concatenate(
            [nt(tokt[at, :], own_map), nt(tokt[at, :], grads[vals:width, :])], axis=1
        )
        for a in range(many):
            for t in range(zeros):
                first = (a * zeros + t) * block
                wbuf[t, a % 2, q * (many // 2) + a // 2] = product[first : first + block].astype(BF16)
        return carry

    lax.fori_loop(0, seqs // many, weigh, 0)

    def back_flow(way, t, p):
        landed = rflow if way == 0 else lflow
        peer = up_peer if way == 0 else down_peer
        return remote(wbuf.at[t, p], landed.at[t, p], rsem.at[way, 0, t, p], rsem.at[way, 1, t, p], peer)

    for z, way in ((0, 0), (last_z, 1)):
        if zeros > 1:
            @pl.when(me_z == z)
            def _():
                for i in range(last_z):
                    for p in (0, 1):
                        back_flow(way, last_z - i if way == 0 else i, p).start()

    wide_head = hmine.shape[1]
    place_row = lax.broadcasted_iota(jnp.int32, (slots, wide_head), 0)
    place = jnp.logical_and(
        lax.broadcasted_iota(jnp.int32, (slots, wide_head), 1) == me_s * hp + place_row, place_row < hp
    )
    lines = [
        jnp.sum(
            jnp.where(place, jnp.sum(acc[i], axis=1, keepdims=True), 0.0), axis=0, keepdims=True
        )
        for i in range(3)
    ]
    hmine[...] = jnp.concatenate(lines + [jnp.zeros((5, wide_head), F32)], axis=0)
    hin[me_z] = hmine[...]

    def head_copy(d):
        return remote(
            hmine, hin.at[me_z], hsem.at[0, d], hsem.at[1, d], (me_s, lax.rem(me_z + d, zeros))
        )

    for d in range(1, zeros):
        head_copy(d).start()

    def turn_of(n):
        return lax.rem(chip + 1 + n, chips)

    def give(i):
        return remote(part.at[i, 1 - core], got_part.at[i], dsem.at[0, i], dsem.at[1, i], sibling)

    def token_send(i):
        return remote(
            sent.at[i], tok_in.at[chip], ksem.at[0, i], ksem.at[1, chip], (i * 2 + core, me_z)
        )

    def settle(n):
        i = turn_of(n)
        give(i).wait_recv()

        def add(j, carry):
            at = pl.ds(pl.multiple_of(j * 128, 128), 128)
            sent[i, at, :] = (part[i, core, at, :] + got_part[i, at, :]).astype(BF16)
            return carry

        lax.fori_loop(0, model // 128, add, 0)

        @pl.when(i != chip)
        def _():
            token_send(i).start()

    def back_project(n, carry):
        i = turn_of(n)
        cols = pl.ds(pl.multiple_of(i * pairs, pairs), pairs)

        def strip_of(j, inner_carry):
            at = pl.ds(pl.multiple_of(j * (model // 2), model // 2), model // 2)
            product = nn(wall[at, :], grads[:, cols])
            part[i, 0, at, :] = product[:, :group]
            part[i, 1, at, :] = product[:, group:]
            return inner_carry

        lax.fori_loop(0, 2, strip_of, 0)
        give(i).start()

        @pl.when(n > 0)
        def _():
            settle(n - 1)
        return carry

    lax.fori_loop(0, chips, back_project, 0)
    settle(chips - 1)

    def along(s):
        return remote(
            zsend.at[s], rows_in.at[me_s], wsem.at[0, s], wsem.at[1, me_s], (s, me_z)
        )

    def events(z):
        found = []
        for i in range(last_z):
            for p in (0, 1):
                for way in (0, 1):
                    t = last_z - i if way == 0 else i
                    if (way == 0 and 0 < z < t) or (way == 1 and t < z < last_z):
                        hops = z if way == 0 else last_z - z
                        found.append((2 * i + p + 3 * hops, p, way, t))
        return sorted(found)

    for z in range(zeros):
        @pl.when(me_z == z)
        def _():
            for _, p, way, t in events(z):
                landed = rflow if way == 0 else lflow
                back_flow(way, t, p).wait_recv()

                def add(j, carry):
                    wbuf[t, p, j] = (wbuf[t, p, j].astype(F32) + landed[t, p, j].astype(F32)).astype(BF16)
                    return carry

                lax.fori_loop(0, seqs // 2, add, 0)
                back_flow(way, t, p).start()
            for p in (0, 1):
                if z > 0:
                    back_flow(0, z, p).wait_recv()
                if z < last_z:
                    back_flow(1, z, p).wait_recv()

                def close(j, carry):
                    value = wbuf[z, p, j].astype(F32)
                    if z > 0:
                        value = value + rflow[z, p, j].astype(F32)
                    if z < last_z:
                        value = value + lflow[z, p, j].astype(F32)
                    zsend[2 * j + p] = value.astype(BF16)
                    return carry

                lax.fori_loop(0, seqs // 2, close, 0)
                for j in range(seqs // 2):
                    @pl.when(me_s != 2 * j + p)
                    def _():
                        along(2 * j + p).start()

    rows_in[me_s] = zsend[me_s]
    for d in range(1, zeros):
        head_copy(d).wait_recv()
    sums = hin[0]
    for d in range(1, zeros):
        sums = sums + hin[d]
    hsum[...] = sums
    hall[me_s] = sums

    def head_along(d):
        return remote(
            hsum, hall.at[me_s], gsem.at[0, d], gsem.at[1, d], (lax.rem(me_s + d, seqs), me_z)
        )

    for d in range(1, seqs):
        head_along(d).start()

    for d in range(1, chips):
        at = lax.rem(chip + d, chips)
        remote(
            sent.at[at], tok_in.at[at], ksem.at[0, at], ksem.at[1, at], (at * 2 + core, me_z)
        ).wait_recv()
    tok_in[chip] = sent[chip]

    def finish(j, carry):
        at = pl.ds(pl.multiple_of(j * 128, 128), 128)
        value = tok_in[0, at, :].astype(F32)
        for c in range(1, chips):
            value = value + tok_in[c, at, :].astype(F32)
        hid[:, at] = value.T.astype(BF16)
        return carry

    lax.fori_loop(0, model // 128, finish, 0)

    for d in range(1, seqs):
        at = lax.rem(me_s + d, seqs)
        remote(
            zsend.at[at], rows_in.at[at], wsem.at[0, at], wsem.at[1, at], (at, me_z)
        ).wait_recv()
        head_along(d).wait_recv()
    map_sums = [jnp.zeros((block, STATE), F32), jnp.zeros((block, STATE), F32)]
    for s in range(seqs):
        piece_in = rows_in[s].astype(F32)
        rows_out[:, s * inner : (s + 1) * inner] = piece_in[:, vals:top]
        rows_out[:, full + 2 * STATE + s * hp : full + 2 * STATE + (s + 1) * hp] = piece_in[:, top : top + hp]
        map_sums[s % 2] = map_sums[s % 2] + piece_in[:, :STATE]
    rows_out[:, full : full + 2 * STATE] = jnp.concatenate(map_sums, axis=1)
    sums = hall[0]
    for s in range(1, seqs):
        sums = sums + hall[s]
    head_out[...] = sums[:3, :heads]

    for p in (0, 1):
        for way in (0, 1):
            for h in range(last_z):
                @pl.when(sends(way, h))
                def _():
                    flow(way, h, p, 0).wait_send()
            for t in range(zeros):
                ahead = me_z < t if way == 0 else me_z > t

                @pl.when(ahead)
                def _():
                    back_flow(way, t, p).wait_send()
    for j in range(zeros):
        shared(j).wait_send()
    for copy in direct + to_sibling + cots:
        copy.wait_send()
    for k in range(chunks):
        map_copy(k).wait_send()
    for i in range(chips):
        give(i).wait_send()

        @pl.when(i != chip)
        def _():
            token_send(i).wait_send()
    for d in range(1, zeros):
        head_copy(d).wait_send()
    for d in range(1, seqs):
        head_along(d).wait_send()
    for s in range(seqs):
        @pl.when(me_s != s)
        def _():
            along(s).wait_send()


def mixer_backward(hidden, cotangent, weight, bias, log, gain, seqs, zeros, hp):
    length, model = hidden.shape
    rows = weight.shape[0]
    heads = bias.shape[1]
    inner = hp * HEAD_DIM
    slots = up(hp, 8)
    width = up(STATE + inner + 16, 128)
    block = rows // seqs
    chips = seqs // 2
    wide = width + STATE
    total = seqs * length
    full = seqs * inner
    span = up(inner + (HEAD_DIM if hp % 2 else 0), 128)
    lanes = up(heads, 128)
    dma = pltpu.SemaphoreType.DMA
    vmem = pl.BlockSpec(memory_space=pltpu.VMEM)
    anywhere = pl.BlockSpec(memory_space=pl.ANY)
    return pl.pallas_call(
        functools.partial(mixer_backward_kernel, seqs, zeros, hp),
        out_shape=(
            jax.ShapeDtypeStruct((length, model), BF16),
            jax.ShapeDtypeStruct((block, full + 2 * STATE + heads), F32),
            jax.ShapeDtypeStruct((3, heads), F32),
        ),
        in_specs=[anywhere] * 3 + [vmem] * 3,
        out_specs=(vmem,) * 3,
        scratch_shapes=[
            pltpu.VMEM((rows, span), BF16),
            pltpu.VMEM((rows, heads), BF16),
            pltpu.VMEM((length, full), BF16),
            pltpu.VMEM((full, length), BF16),
            pltpu.VMEM((seqs, length, model), BF16),
            pltpu.VMEM((model, total), BF16),
            pltpu.VMEM((model, wide), BF16),
            pltpu.VMEM((zeros, wide, rows), BF16),
            pltpu.VMEM((wide, total), F32),
            pltpu.VMEM((seqs, inner, length), BF16),
            pltpu.VMEM((seqs, inner, length), F32),
            pltpu.VMEM((seqs, inner, length), BF16),
            pltpu.VMEM((seqs + 1, inner, STATE), BF16),
            pltpu.VMEM((wide, total), BF16),
            pltpu.VMEM((inner, STATE), F32),
            pltpu.VMEM((3, slots, length), F32),
            pltpu.VMEM((seqs * slots, length), F32),
            pltpu.VMEM((seqs * slots, length), F32),
            pltpu.VMEM((seqs, length, length), F32),
            pltpu.VMEM((seqs * slots, length), F32),
            pltpu.VMEM((2, seqs, STATE, length), F32),
            pltpu.VMEM((seqs, STATE, length), F32),
            pltpu.VMEM((chips, 2, model, length), F32),
            pltpu.VMEM((chips, model, length), F32),
            pltpu.VMEM((chips, model, length), BF16),
            pltpu.VMEM((chips, model, length), BF16),
            pltpu.VMEM((zeros, 2, seqs // 2, block, width), BF16),
            pltpu.VMEM((zeros, 2, seqs // 2, block, width), BF16),
            pltpu.VMEM((zeros, 2, seqs // 2, block, width), BF16),
            pltpu.VMEM((seqs, block, width), BF16),
            pltpu.VMEM((seqs, block, width), BF16),
            pltpu.VMEM((zeros, 8, lanes), F32),
            pltpu.VMEM((8, lanes), F32),
            pltpu.VMEM((8, lanes), F32),
            pltpu.VMEM((seqs, 8, lanes), F32),
            dma((2, 2, zeros + 1, 2)),
            dma((2, seqs)),
            dma((2, seqs)),
            dma((2, seqs)),
            dma((2, zeros)),
            dma((2, seqs)),
            dma((2, chips)),
            dma((2, chips)),
            dma((2, 2, zeros, 2)),
            dma((2, seqs)),
            dma((2, zeros)),
            dma((2, seqs)),
            dma((5,)),
        ],
        compiler_params=pltpu.CompilerParams(
            collective_id=0, has_side_effects=True, vmem_limit_bytes=60 * 1024 * 1024
        ),
        name="mixer_backward",
    )(hidden, cotangent, weight, bias, log, gain)


def body(seqs, zeros, hidden, output_grad, input_weight, step_bias, decay_log, skip_gain):
    heads = step_bias.shape[0]
    hp = up(heads, seqs) // seqs
    spare = seqs * hp - heads
    full, total = heads * HEAD_DIM, seqs * hp * HEAD_DIM
    tokens, cot, weight = hidden[0], output_grad[0], input_weight
    params = [step_bias, decay_log, skip_gain]
    if spare:
        cot = jnp.pad(cot, ((0, 0), (0, total - full)))
        gap = jnp.zeros((weight.shape[0], total - full), BF16)
        few = jnp.zeros((weight.shape[0], spare), BF16)
        weight = jnp.concatenate([weight[:, :full], gap, weight[:, full:], few], axis=1)
        params = [jnp.pad(v, (0, spare)) for v in params]
    token_grad, weight_grad, head_grads = mixer_backward(
        tokens, cot, weight, *[v[None] for v in params], seqs, zeros, hp
    )
    if spare:
        weight_grad = jnp.concatenate(
            [weight_grad[:, :full], weight_grad[:, total : total + 2 * STATE + heads]], axis=1
        )
        head_grads = head_grads[:, :heads]
    return (token_grad[None], weight_grad, head_grads)


def solution(mesh):
    placed = (P("zero", "seq", None), P("zero", "seq", None), P("zero", None), P(), P(), P())
    return jax.shard_map(
        functools.partial(body, mesh.shape["seq"], mesh.shape["zero"]),
        mesh=mesh,
        in_specs=placed,
        out_specs=(P("zero", "seq", None), P(("seq", "zero"), None), P()),
        check_vma=False,
    )
```

time: 121 us -> 82.4 us (0.68)
  the two profiles are of different devices: /device:TPU:9 before, /device:TPU:0 now
where the time goes in v1:
time: 82.4 us; the launch traced here: 82.1 us
  Pallas kernels  76.7 us (93%)
  local copies, waits for them, and re-layouts  4.78 us (6%)
    pallas_call x1, Pallas kernels, mixer_backward(): pl.pallas_call(functools.partial(mixer_backward_kernel, seqs, zeros, hp),...  76.7 us
    unnamed x3, local copies, waits for them, and re-layouts  4.78 us

profile of v1, /device:TPU:0, one launch (start us, length us, event | category | flops | bytes accessed | tf_op | source)
XLA Modules:
  0.0 82.1 jit_solution(13924961033971196043)
XLA Ops:
  0.6 76.7 %mixer_backward.1 = (bf16[128,1280]{1,0:T(8,128)(2,1)}, f32[40,2856]{1,0:T(8,128)}, f32[3,40]{1,0:T(4,128)}) custom-call(bf16[128,1280]{1,0:T(8,128)(2,1)} %bitcast.8, bf16[128,2560]{1,0:T(8,128)(2,1)} %bitcast.6, bf16[320,2856]{1,0:T(8,128)(2,1)} %weight.1, f32[1,40]{1,0:T(1,128)} %bitcast.9, f32[1,40]{1,0:T(1,128)} %bitcast.10, f32[1,40]{1,0:T(1,128)} %bitcast.11), custom_call_target="tpu_custom_call" | custom-call | tf_op jit(solution)/shard_map/mixer_backward/pallas_call | solution.py:691
  77.4 1.7 %copy.12 = bf16[1,128,1280]{2,1,0:T(8,128)(2,1)} copy(bf16[1,128,1280]{2,1,0:T(8,128)(2,1)} %bitcast.7) | data formatting | bytes 655360
  79.1 1.8 %copy.13 = f32[40,2856]{1,0:T(8,128)} copy(f32[40,2856]{1,0:T(8,128)} %get-tuple-element.13) | data formatting | bytes 913920
  80.9 1.2 %copy.14 = f32[3,40]{1,0:T(4,128)} copy(f32[3,40]{1,0:T(4,128)} %get-tuple-element.14) | data formatting | bytes 960

commit v2 on v1

v2 whole, which is shorter than its diff:
```python
import functools

import jax
import jax.numpy as jnp
from jax import lax
from jax.experimental import pallas as pl
from jax.experimental.pallas import tpu as pltpu
from jax.sharding import PartitionSpec as P

HEAD_DIM = 64
STATE = 128
MESH = pl.DeviceIdType.MESH
F32 = jnp.float32
BF16 = jnp.bfloat16


def up(size, unit):
    return -(-size // unit) * unit


def nn(a, b):
    return lax.dot_general(a, b, (((1,), (0,)), ((), ())), preferred_element_type=F32)


def nt(a, b):
    return lax.dot_general(a, b, (((1,), (1,)), ((), ())), preferred_element_type=F32)


def tn(a, b):
    return lax.dot_general(a, b, (((0,), (0,)), ((), ())), preferred_element_type=F32)


def halves(a):
    high = a.astype(BF16)
    return high, (a - high.astype(F32)).astype(BF16)


def remote(src, dst, send, recv, peer):
    return pltpu.make_async_remote_copy(src, dst, send, recv, peer, MESH)


def groups_of(hp):
    first = hp - hp // 2
    second = hp - first
    return (first, up(first * HEAD_DIM + 16, 128)), (second, up(second * HEAD_DIM, 128))


def mixer_backward_kernel(
    seqs, zeros, hp,
    hidden, cotangent, weight, bias_in, log_in, gain_in,
    hid, rows_out, head_out,
    window, tiny, cotv, cott,
    toks, tokt, wall, wallt, pre, dys, xs, tails, states, grads, grad, acc, steps, cums, cumt, sigr,
    maps, got_map, part, got_part, sent, tok_in, wbuf, rflow, lflow, zsend, rows_in, hin, hsum, hmine, hall,
    ins, outs, scores, swbuf, swin, stsend, stin,
    asem, tsem, psem, csem, ssem, msem, dsem, ksem, rsem, gsem, hsem, wsem, loc, ysem, xsem,
):
    me_s, me_z = lax.axis_index("seq"), lax.axis_index("zero")
    chips = seqs // 2
    chip, core = me_s // 2, lax.rem(me_s, 2)
    sib = me_s // 2 * 2 + 1 - core
    sibling = (sib, me_z)
    length, model = hidden.shape
    rows = weight.shape[0]
    wide = wall.shape[1]
    inner = dys.shape[1]
    (n1, w1), (n2, w2) = groups_of(hp)
    in1, in2 = n1 * HEAD_DIM, n2 * HEAD_DIM
    slots = acc.shape[1]
    full = cotangent.shape[1]
    chunks, group = seqs, length
    v1 = 2 * STATE
    top, v2 = v1 + in1, v1 + w1
    extra = wide
    up_peer, down_peer = (me_s, me_z + 1), (me_s, me_z - 1)
    half = rows // 2
    last_z = zeros - 1
    pairs = 2 * group

    peers = [(lax.rem(me_s + d, seqs), me_z) for d in range(1, seqs)]
    peers += [(me_s, lax.rem(me_z + d, zeros)) for d in range(1, zeros)]
    barrier = pltpu.get_barrier_semaphore()
    for peer in peers:
        pl.semaphore_signal(barrier, inc=1, device_id=peer, device_id_type=MESH)

    start = pl.multiple_of(me_s * inner // 128 * 128, 128)
    mine = pl.ds(pl.multiple_of(me_z * rows, rows), rows)
    fetch = [
        pltpu.make_async_copy(weight.at[:, pl.ds(start, window.shape[1])], window, loc.at[0]),
        pltpu.make_async_copy(
            weight.at[:, pl.ds(pl.multiple_of(full + core * STATE, 128), STATE)],
            wall.at[mine, pl.ds(STATE, STATE)], loc.at[1],
        ),
        pltpu.make_async_copy(weight.at[:, pl.ds(full + 2 * STATE, tiny.shape[1])], tiny, loc.at[2]),
        pltpu.make_async_copy(hidden, toks.at[me_s], loc.at[3]),
        pltpu.make_async_copy(cotangent, cotv, loc.at[4]),
    ]
    for copy in fetch:
        copy.start()
    heads = tiny.shape[1]
    head_row = lax.broadcasted_iota(jnp.int32, (heads, v2 - top), 0)
    head_col = lax.broadcasted_iota(jnp.int32, (heads, v2 - top), 1)
    chosen = jnp.logical_and(head_row == me_s * hp + head_col, head_col < hp)
    chosen = jnp.where(chosen, 1.0, 0.0).astype(BF16)
    fetch[2].wait()
    wall[mine, top:v2] = nn(tiny[...], chosen).astype(BF16)
    fetch[0].wait()
    def place_values(shift):
        wall[mine, v1:top] = window[:, shift : shift + in1]
        wall[mine, v2 : v2 + in2] = window[:, shift + in1 : shift + inner]
        if w2 > in2:
            wall[mine, v2 + in2 : v2 + w2] = jnp.zeros((rows, w2 - in2), BF16)

    if hp % 2:
        shifted = lax.rem(me_s, 2)
        for shift in (0, 1):
            @pl.when(shifted == shift)
            def _():
                place_values(shift * HEAD_DIM)
    else:
        place_values(0)
    fetch[1].wait()
    fetch[3].wait()

    pl.semaphore_wait(barrier, len(peers))

    spans = ((STATE, STATE + w1), (v2, w2))

    def piece(g, at, p):
        first = pl.multiple_of(at * rows + p * half, half)
        return wall.at[pl.ds(first, half), pl.ds(*spans[g])]

    def flow(g, way, h, p, recv):
        at = me_z - h if way == 0 else me_z + h
        return remote(
            piece(g, at, p), piece(g, at, p),
            asem.at[g, way, 0, h, p], asem.at[g, way, 1, h + (1 - recv), p],
            up_peer if way == 0 else down_peer,
        )

    def sends(way, h):
        if way == 0:
            return jnp.logical_and(me_z < last_z, me_z >= h)
        return jnp.logical_and(me_z > 0, me_z + h <= last_z)

    def comes(way, h):
        return me_z >= h if way == 0 else me_z + h <= last_z

    def shared(at):
        first = pl.multiple_of(at * rows, rows)
        return remote(
            wall.at[pl.ds(first, rows), pl.ds(STATE, STATE)],
            wall.at[pl.ds(first, rows), pl.ds(0, STATE)],
            ssem.at[0, at], ssem.at[1, at], sibling,
        )

    for p in (0, 1):
        for way in (0, 1):
            @pl.when(sends(way, 0))
            def _():
                flow(0, way, 0, p, 0).start()

    def own_late(h):
        for way in (0, 1):
            distance = me_z if way == 0 else last_z - me_z

            @pl.when(jnp.logical_and(distance == h, sends(way, 0)))
            def _():
                for p in (0, 1):
                    flow(1, way, 0, p, 0).start()

    own_late(0)

    def token(src_s, dst, lo, size, slot):
        block = toks.at[src_s, pl.ds(lo, size)]
        return remote(block, block, tsem.at[0, slot], tsem.at[1, slot], (dst, me_z))

    def passed(src_s, slot):
        return remote(toks.at[src_s], toks.at[src_s], psem.at[0, slot], psem.at[1, slot], sibling)

    square = chips == 4
    cut = length // 2
    to_sibling = [passed(me_s, 0)]
    if square:
        flat = chip + 1 - 2 * lax.rem(chip, 2)
        tall = lax.rem(chip + 2, 4)
        far = lax.rem(flat + 2, 4)
        around = [flat, tall]
    else:
        around = [lax.rem(chip + d, chips) for d in range(1, chips)]
    direct = [token(me_s, c * 2 + core, 0, length, i) for i, c in enumerate(around)]
    for copy in direct + to_sibling:
        copy.start()
    shared(me_z).start()

    pre[...] = jnp.zeros_like(pre)
    fetch[4].wait()
    strip = 512

    def turn_cot(j, carry):
        at = pl.ds(pl.multiple_of(j * strip, strip), strip)
        cott[at, :] = cotv[:, at].T
        return carry

    lax.fori_loop(0, full // strip, turn_cot, 0)

    def cot_of(s):
        return cott.at[pl.ds(pl.multiple_of(s * inner, inner), inner)]

    dys[me_s] = cot_of(me_s)[...]

    def step_hop(h):
        for p in (0, 1):
            for way in (0, 1):
                @pl.when(comes(way, h))
                def _():
                    flow(0, way, h, p, 1).wait_recv()
                if h < last_z:
                    @pl.when(sends(way, h))
                    def _():
                        flow(0, way, h, p, 0).start()
        if h < last_z:
            own_late(h)
        for way in (0, 1):
            @pl.when(comes(way, h))
            def _():
                shared(me_z - h if way == 0 else me_z + h).start()

    def late_hop(h, onward):
        for p in (0, 1):
            for way in (0, 1):
                goes = sends(way, h) if h < last_z else jnp.bool_(False)
                if onward:
                    if h < last_z:
                        @pl.when(goes)
                        def _():
                            flow(1, way, h, p, 1).wait_recv()
                            flow(1, way, h, p, 0).start()
                else:
                    @pl.when(jnp.logical_and(comes(way, h), jnp.logical_not(goes)))
                    def _():
                        flow(1, way, h, p, 1).wait_recv()

    if zeros > 2:
        step_hop(1)

    def chip_of(n):
        if square:
            return lax.rem(chip // 2 + n // 2, 2) * 2 + lax.rem(lax.rem(chip, 2) + n % 2, 2)
        return lax.rem(chip + n, chips)

    def turn(n, carry):
        for half_chip in (0, 1):
            k = chip_of(n) * 2 + half_chip
            tokt[:, pl.ds(pl.multiple_of(k * group, group), group)] = toks[k].T
        return carry

    early = 3 if square else 0
    if square:
        onward = [
            token(flat * 2 + core, tall * 2 + core, 0, cut, 2),
            token(tall * 2 + core, flat * 2 + core, cut, length - cut, 3),
        ]
        for i in (0, 1):
            direct[i].wait_recv()
            onward[i].start()
        direct += onward
        more = [passed(flat * 2 + core, 1), passed(tall * 2 + core, 2)]
        for copy in more:
            copy.start()
        to_sibling += more
        for copy in to_sibling:
            copy.wait_recv()
        lax.fori_loop(0, early, turn, 0)

    for h in range(2, last_z):
        step_hop(h)

    def flip(j):
        shared(j).wait_recv()
        wallt[j] = wall[pl.ds(pl.multiple_of(j * rows, rows), rows), :v2].T

    def project(j, first, final):
        def part_of(n, carry):
            at = pl.ds(pl.multiple_of(j * rows, rows), rows)
            cols = pl.ds(pl.multiple_of(chip_of(n) * pairs, pairs), pairs)
            pre[:v2, cols] += nn(wallt[j], tokt[at, cols])
            return carry

        lax.fori_loop(first, final, part_of, 0)

    def near(first, final, fresh):
        def one(j, carry):
            distance = jnp.abs(j - me_z)
            ready = distance < last_z if zeros > 1 else distance < 1

            @pl.when(ready)
            def _():
                if fresh:
                    flip(j)
                project(j, first, final)
            return carry

        lax.fori_loop(0, zeros, one, 0)

    if early:
        near(0, early, True)

    if square:
        token(far * 2 + core, tall * 2 + core, 0, cut, 2).wait_recv()
        token(far * 2 + core, flat * 2 + core, cut, length - cut, 3).wait_recv()
        rest = [passed(far * 2 + core, 3)]
    else:
        rest = []
        for d in range(1, chips):
            direct[d - 1].wait_recv()
            rest.append(passed(lax.rem(chip - d + chips, chips) * 2 + core, d))
    for copy in rest:
        copy.start()
    cots = []
    for d in range(1, seqs):
        peer = lax.rem(me_s + d, seqs)
        cots.append(remote(cot_of(peer), dys.at[me_s], csem.at[0, d], csem.at[1, d], (peer, me_z)))
    for copy in cots:
        copy.start()
    if not square:
        rest = to_sibling + rest
    for copy in rest:
        copy.wait_recv()
    to_sibling = to_sibling + rest if square else rest
    lax.fori_loop(early, chips, turn, 0)
    near(early, chips, not early)

    batch = 4 * group if chunks % 4 == 0 else pairs

    if zeros > 2:
        late_hop(1, True)
    if zeros > 1:
        step_hop(last_z)
        far_end = jnp.logical_or(me_z == 0, me_z == last_z)

        @pl.when(far_end)
        def _():
            flip(last_z - me_z)
            project(last_z - me_z, 0, chips)

    in_at = pl.multiple_of((1 - core) * STATE, 128)
    out_at = pl.multiple_of(core * STATE, 128)
    slot = lax.broadcasted_iota(jnp.int32, (slots, heads), 0)
    own_head = jnp.logical_and(
        lax.broadcasted_iota(jnp.int32, (slots, heads), 1) == me_s * hp + slot, slot < hp
    )

    def own(ref):
        return jnp.sum(jnp.where(own_head, ref[...], 0.0), axis=1, keepdims=True)

    bias, rate, gain = own(bias_in), -jnp.exp(own(log_in)), own(gain_in)
    row = lax.broadcasted_iota(jnp.int32, (group, group), 0)
    col = lax.broadcasted_iota(jnp.int32, (group, group), 1)
    causal = col >= row

    def spread(values, span):
        return jnp.concatenate(
            [jnp.broadcast_to(values[h : h + 1], (HEAD_DIM, values.shape[1])) for h in span], axis=0
        )

    def gather_rows(whole, span):
        parts = [
            jnp.sum(whole[i * HEAD_DIM : (i + 1) * HEAD_DIM], axis=0, keepdims=True)
            for i in range(len(span))
        ]
        return padded(parts, span)

    def padded(parts, span):
        lanes = parts[0].shape[1]
        if span[0] > 0:
            parts = [jnp.zeros((span[0], lanes), F32)] + parts
        if slots > span[-1] + 1:
            parts = parts + [jnp.zeros((slots - span[-1] - 1, lanes), F32)]
        return jnp.concatenate(parts, axis=0)

    raw = pre[top : top + slots, :] + bias
    soft = jax.nn.softplus(raw)
    curve = jax.nn.sigmoid(raw)
    stacked = jnp.concatenate([soft[:, k * group : (k + 1) * group] for k in range(chunks)], axis=0)
    steps[...] = stacked
    sigr[...] = jnp.concatenate([curve[:, k * group : (k + 1) * group] for k in range(chunks)], axis=0)
    logs = jnp.concatenate([rate] * chunks, axis=0) * stacked
    before = jnp.where(causal, 1.0, 0.0).astype(BF16)
    after = jnp.where(col <= row, 1.0, 0.0).astype(BF16)

    def summed(values, mask):
        a = values.astype(BF16)
        rest = values - a.astype(F32)
        b = rest.astype(BF16)
        c = (rest - b.astype(F32)).astype(BF16)
        return nn(a, mask) + (nn(b, mask) + nn(c, mask))

    cums[...] = summed(logs, before)

    def small(ref, k):
        return ref[pl.ds(pl.multiple_of(k * slots, slots), slots), :]

    def forward(g, k):
        span, mine_v, size = (range(n1), v1, in1) if g == 0 else (range(n1, hp), v2, in2)
        here = slice(span[0] * HEAD_DIM, span[0] * HEAD_DIM + size)
        at = pl.ds(pl.multiple_of(k * group, group), group)
        p = pre[mine_v : mine_v + size, at]
        sig = jax.nn.sigmoid(p)
        x = p * sig
        xs[k, here] = x
        pre[mine_v : mine_v + size, at] = sig * (1.0 + p * (1.0 - sig))
        step, cum = small(steps, k), small(cums, k)
        last = cum[:, group - 1 :]
        if g == 0:
            m_in, m_out = pre[pl.ds(in_at, STATE), at], pre[pl.ds(out_at, STATE), at]
            in16 = (m_in * jax.nn.sigmoid(m_in)).astype(BF16)
            out16 = (m_out * jax.nn.sigmoid(m_out)).astype(BF16)
            ins[k] = in16
            outs[k] = out16
            scores[k] = tn(in16, out16)
            cumt[k] = jnp.concatenate([cum, jnp.zeros((group - slots, group), F32)], axis=0).T
        else:
            in16 = ins[k]
        tail16 = (x * spread(step * jnp.exp(last - cum), span)).astype(BF16)
        tails[k, here] = tail16
        held = grad[here]
        states[k, here] = held.astype(BF16)
        leave = spread(jnp.exp(jnp.broadcast_to(last, (slots, STATE))), span)
        grad[here] = leave * held + nt(tail16, in16)

    def map_copy(k):
        return remote(maps.at[1 - core, k], got_map.at[k], msem.at[0, k], msem.at[1, k], sibling)

    def backward(g, k):
        span, mine_v, size = (range(n1), v1, in1) if g == 0 else (range(n1, hp), v2, in2)
        here = slice(span[0] * HEAD_DIM, span[0] * HEAD_DIM + size)
        at = pl.ds(pl.multiple_of(k * group, group), group)
        step, cum = small(steps, k), small(cums, k)
        last = cum[:, group - 1 :]
        x = xs[k, here]
        step_full = spread(step, span)
        u16 = (x * step_full).astype(BF16)
        tail16 = tails[k, here]
        in16, out16 = ins[k], outs[k]
        dy16 = dys[k, here]
        dy = dy16.astype(F32)
        tail = spread(jnp.exp(last - cum), span)
        lead = spread(jnp.exp(cum), span)
        leave = spread(jnp.exp(jnp.broadcast_to(last, (slots, STATE))), span)
        held16 = states[k, here]
        g_out = grad[here]
        g16 = g_out.astype(BF16)
        dy_lead = dy * lead
        lead16 = dy_lead.astype(BF16)

        score = scores[k]
        cum_col = cumt[k]
        d_score = jnp.zeros((group, group), F32)
        du_parts, r_parts = [], []
        for i, h in enumerate(span):
            at_h = slice(i * HEAD_DIM, (i + 1) * HEAD_DIM)
            diff = cum[h : h + 1] - cum_col[:, h : h + 1]
            within = jnp.exp(jnp.where(causal, diff, -1e30))
            mixing = (score * within).astype(BF16)
            d_mix = tn(u16[at_h], dy16[at_h])
            du_parts.append(nt(dy16[at_h], mixing))
            d_score = d_score + d_mix * within
            r_parts.append(jnp.sum(d_mix * mixing.astype(F32), axis=0, keepdims=True))
        du = jnp.concatenate(du_parts, axis=0) + nn(g16, in16) * tail
        from_x = gather_rows(du * x, span)
        from_u = gather_rows(du * u16.astype(F32), span)
        lead_rows = gather_rows(dy_lead * nn(held16, out16), span)
        cross = jnp.sum(gather_rows(g_out * states[k + 1, here].astype(F32), span), axis=1, keepdims=True)
        d_cum = padded(r_parts, span) + lead_rows - from_u
        d_log = summed(d_cum, after) + cross
        d_raw = (from_x + rate * d_log) * small(sigr, k)

        d_score16 = d_score.astype(BF16)
        d_out = nn(in16, d_score16) + tn(held16, lead16)
        d_in = nt(out16, d_score16) + tn(g16, tail16)
        grad[here] = leave * g_out + nt(lead16, out16)
        slope = pre[mine_v : mine_v + size, at]
        gain_full = spread(jnp.broadcast_to(gain, (slots, group)), span)
        grads[mine_v : mine_v + size, at] = ((du * step_full + dy * gain_full) * slope).astype(BF16)
        fill = jnp.zeros((16 - slots, group), F32)
        raw16 = jnp.concatenate([d_raw, fill], axis=0).astype(BF16)
        acc[0] += d_raw
        acc[1] += d_log * (rate * step)
        acc[2] += gather_rows(dy * x, span)
        if g == 0:
            grads[top : top + 16, at] = raw16
            maps[0, k] = d_in
            maps[1, k] = d_out
        else:
            grads[top : top + 16, at] += raw16
            m_in, m_out = pre[pl.ds(in_at, STATE), at], pre[pl.ds(out_at, STATE), at]
            s_in, s_out = jax.nn.sigmoid(m_in), jax.nn.sigmoid(m_out)
            d_in = (maps[0, k] + d_in) * (s_in * (1.0 + m_in * (1.0 - s_in)))
            d_out = (maps[1, k] + d_out) * (s_out * (1.0 + m_out * (1.0 - s_out)))
            maps[0, k] = d_in
            maps[1, k] = d_out
            grads[pl.ds(in_at, STATE), at] = d_in.astype(BF16)
            grads[pl.ds(out_at, STATE), at] = d_out.astype(BF16)
            map_copy(k).start()

    def both_ways(g):
        def ahead(k, carry):
            forward(g, k)
            return carry

        def back(n, carry):
            backward(g, chunks - 1 - n)
            return carry

        here = slice(0, in1) if g == 0 else slice(in1, inner)
        lax.fori_loop(0, chunks, ahead, 0)
        states[chunks, here] = grad[here].astype(BF16)
        grad[here] = jnp.zeros_like(grad[here])
        if g == 0:
            for h in range(2, last_z):
                late_hop(h, True)
            for copy in cots:
                copy.wait_recv()
        if g == 0:
            lax.fori_loop(0, chunks, back, 0)
        else:
            lax.fori_loop(0, chunks // 2, back, 0)
            serve(0, 1)
            lax.fori_loop(chunks // 2, chunks, back, 0)

    block = wbuf.shape[4]
    many = 4 if seqs % 4 == 0 else 2
    span_rows = many * zeros * block

    def weigh(g, first, size):
        def part_of(q, carry):
            at = pl.ds(pl.multiple_of(q * span_rows, span_rows), span_rows)
            product = nt(tokt[at, :], grads[first : first + size, :])
            for a in range(many):
                for t in range(zeros):
                    lo = (a * zeros + t) * block
                    wbuf[g, t, a % 2, q * (many // 2) + a // 2, :, 0:size] = product[
                        lo : lo + block
                    ].astype(BF16)
            return carry

        lax.fori_loop(0, seqs // many, part_of, 0)

    sizes = (w1, w2 + STATE)

    def back_flow(g, way, t, p):
        landed = rflow if way == 0 else lflow
        peer = up_peer if way == 0 else down_peer
        return remote(
            wbuf.at[g, t, p, :, :, pl.ds(0, sizes[g])], landed.at[g, t, p, :, :, pl.ds(0, sizes[g])],
            rsem.at[g, way, 0, t, p], rsem.at[g, way, 1, t, p], peer,
        )

    def from_ends(g):
        for z, way in ((0, 0), (last_z, 1)):
            if zeros > 1:
                @pl.when(me_z == z)
                def _():
                    for i in range(last_z):
                        for p in (0, 1):
                            back_flow(g, way, last_z - i if way == 0 else i, p).start()

    low = model // 2

    def turn_of(n):
        return lax.rem(chip + 1 + n, chips)

    def give(i, j):
        at = pl.ds(j * low, low)
        return remote(
            part.at[i, 1 - core, at], got_part.at[i, at], dsem.at[0, i, j], dsem.at[1, i, j], sibling
        )

    def token_send(i):
        return remote(
            sent.at[i], tok_in.at[chip], ksem.at[0, i], ksem.at[1, chip], (i * 2 + core, me_z)
        )

    def settle(n):
        i = turn_of(n)
        for j in (0, 1):
            at = slice(j * low, (j + 1) * low)
            give(i, j).wait_recv()
            sent[i, at, :] = (part[i, core, at, :] + got_part[i, at, :]).astype(BF16)

        @pl.when(i != chip)
        def _():
            token_send(i).start()

    def events(z):
        found = []
        for g in (0, 1):
            for p in (0, 1):
                ends = 0.0
                for i in range(last_z):
                    for way in (0, 1):
                        t = last_z - i if way == 0 else i
                        hops = z if way == 0 else last_z - z
                        if hops == 0:
                            continue
                        when = (g * last_z + i) * 2 + p + 1 + 2.2 * hops
                        if t == z:
                            ends = max(ends, when)
                        elif (way == 0) == (z < t):
                            found.append((when, 1 + g, "pass", (way, t, p)))
                found.append((ends + 0.01, 1 + g, "end", p))
            if g == 0:
                found.append((ends + 0.02, 1, "heads", 0))
        return sorted(found, key=lambda e: e[:2])

    served = 4

    def serve(first, final):
        for z in range(zeros):
            listed = events(z)
            soon = [e for e in listed if e[1:3] == (1, "pass")][:served]
            todo = [e for e in listed if e not in soon] if final is None else soon[first:final]
            if todo:
                @pl.when(me_z == z)
                def _():
                    serve_at(z, todo)

    def serve_at(z, todo):
        for _, g, what, p in todo:
            g = g - 1
            if what == "pass":
                way, t, p = p
                landed = rflow if way == 0 else lflow
                back_flow(g, way, t, p).wait_recv()
                wbuf[g, t, p] = (
                    wbuf[g, t, p].astype(F32) + landed[g, t, p].astype(F32)
                ).astype(BF16)
                back_flow(g, way, t, p).start()
            elif what == "heads":
                close_heads()
                drain()
            else:
                finish_piece(z, g, p)

    def head_copy(d):
        return remote(
            hmine, hin.at[me_z], hsem.at[0, d], hsem.at[1, d], (me_s, lax.rem(me_z + d, zeros))
        )

    def head_along(d):
        return remote(
            hsum, hall.at[me_s], gsem.at[0, d], gsem.at[1, d], (lax.rem(me_s + d, seqs), me_z)
        )

    def close_heads():
        for d in range(1, zeros):
            head_copy(d).wait_recv()
        sums = hin[0]
        for d in range(1, zeros):
            sums = sums + hin[d]
        hsum[...] = sums
        hall[me_s] = sums
        for d in range(1, seqs):
            head_along(d).start()

    def drain():
        for g in (0, 1):
            for p in (0, 1):
                for way in (0, 1):
                    for h in range(last_z):
                        @pl.when(sends(way, h))
                        def _():
                            flow(g, way, h, p, 0).wait_send()
        for j in range(zeros):
            shared(j).wait_send()
        for copy in direct + to_sibling + cots:
            copy.wait_send()

        def gone(k, carry):
            map_copy(k).wait_send()
            return carry

        lax.fori_loop(0, chunks, gone, 0)
        for i in range(chips):
            for j in (0, 1):
                give(i, j).wait_send()

    def finish_piece(z, g, p):
        if z > 0:
            back_flow(g, 0, z, p).wait_recv()
        if z < last_z:
            back_flow(g, 1, z, p).wait_recv()
        if g == 1 and p == 0:
            for d in range(1, zeros):
                steps_copy(d).wait_recv()
            total = swin[0].astype(F32)
            for d in range(1, zeros):
                total = total + swin[d].astype(F32)
            total = total.astype(BF16)
            for s in range(seqs):
                stsend[s] = total[:, s * 16 : (s + 1) * 16]
            for s in range(seqs):
                @pl.when(me_s != s)
                def _():
                    steps_along(s).start()
        for j in range(seqs // 2):
            s = 2 * j + p
            value = wbuf[g, z, p, j, :, 0 : sizes[g]].astype(F32)
            if z > 0:
                value = value + rflow[g, z, p, j, :, 0 : sizes[g]].astype(F32)
            if z < last_z:
                value = value + lflow[g, z, p, j, :, 0 : sizes[g]].astype(F32)
            zsend[g, s, :, 0 : sizes[g]] = value.astype(BF16)
        for j in range(seqs // 2):
            @pl.when(me_s != 2 * j + p)
            def _():
                along(g, 2 * j + p).start()

    def along(g, s):
        lanes = pl.ds(0, sizes[g])
        return remote(
            zsend.at[g, s, :, lanes], rows_in.at[g, me_s, :, lanes],
            wsem.at[g, 0, s], wsem.at[g, 1, me_s], (s, me_z),
        )

    def steps_along(s):
        return remote(stsend.at[s], stin.at[me_s], xsem.at[0, s], xsem.at[1, me_s], (s, me_z))

    def steps_copy(d):
        target = lax.rem(me_z + d, zeros)
        return remote(
            swbuf.at[target], swin.at[me_z], ysem.at[0, d], ysem.at[1, d], (me_s, target)
        )

    grad[...] = jnp.zeros_like(grad)
    acc[...] = jnp.zeros_like(acc)
    grads[pl.ds(top, v2 - top), :] = jnp.zeros((v2 - top, chunks * group), BF16)
    if w2 > in2:
        grads[pl.ds(v2 + in2, w2 - in2), :] = jnp.zeros((w2 - in2, chunks * group), BF16)
    both_ways(0)
    weigh(0, v1, w1)
    from_ends(0)

    for h in range(1, zeros):
        late_hop(h, False)

    def project_late(i, carry):
        cols = pl.ds(pl.multiple_of(i * batch, batch), batch)
        pre[v2:wide, cols] = tn(wall[:, v2:wide], tokt[:, cols])
        return carry

    lax.fori_loop(0, chunks * group // batch, project_late, 0)
    both_ways(1)
    serve(1, 2)

    for j in (0, 1):
        at = slice(j * low, (j + 1) * low)
        product = nn(wall[at, :], grads[0:wide, :])
        for k in range(chunks):
            part[k // 2, k % 2, at, :] = product[:, k * group : (k + 1) * group]
        for n in range(chips):
            give(turn_of(n), j).start()
        serve(2 + j, 3 + j)

    def merge(k, carry):
        map_copy(k).wait_recv()
        at = pl.ds(pl.multiple_of(k * group, group), group)
        grads[extra : extra + STATE, at] = (maps[core, k] + got_map[k]).astype(BF16)
        return carry

    lax.fori_loop(0, chunks, merge, 0)
    wide_head = hmine.shape[1]
    place_row = lax.broadcasted_iota(jnp.int32, (slots, wide_head), 0)
    place = jnp.logical_and(
        lax.broadcasted_iota(jnp.int32, (slots, wide_head), 1) == me_s * hp + place_row, place_row < hp
    )
    lines = [
        jnp.sum(
            jnp.where(place, jnp.sum(acc[i], axis=1, keepdims=True), 0.0), axis=0, keepdims=True
        )
        for i in range(3)
    ]
    hmine[...] = jnp.concatenate(lines + [jnp.zeros((5, wide_head), F32)], axis=0)
    hin[me_z] = hmine[...]

    for d in range(1, zeros):
        head_copy(d).start()

    weigh(1, v2, w2 + STATE)
    from_ends(1)

    steps_grad = nt(tokt[...], grads[top : top + 16, :])
    for t in range(zeros):
        lines = [
            steps_grad[(s * zeros + t) * block : (s * zeros + t + 1) * block] for s in range(seqs)
        ]
        swbuf[t] = jnp.concatenate(lines, axis=1).astype(BF16)
    swin[me_z] = swbuf[me_z]

    for d in range(1, zeros):
        steps_copy(d).start()

    for n in range(chips):
        settle(n)
    serve(None, None)

    for g in (0, 1):
        rows_in[g, me_s] = zsend[g, me_s]
    for d in range(1, chips):
        at = lax.rem(chip + d, chips)
        remote(
            sent.at[at], tok_in.at[at], ksem.at[0, at], ksem.at[1, at], (at * 2 + core, me_z)
        ).wait_recv()
    tok_in[chip] = sent[chip]

    for j in (0, 1):
        at = slice(j * low, (j + 1) * low)
        value = tok_in[0, at, :].astype(F32)
        for source in range(1, chips):
            value = value + tok_in[source, at, :].astype(F32)
        hid[:, at] = value.T.astype(BF16)

    def landed_from(g, s):
        @pl.when(me_s != s)
        def _():
            lanes = pl.ds(0, sizes[g])
            remote(
                zsend.at[g, s, :, lanes], rows_in.at[g, s, :, lanes],
                wsem.at[g, 0, s], wsem.at[g, 1, s], (s, me_z),
            ).wait_recv()

    stin[me_s] = stsend[me_s]
    for s in range(seqs):
        @pl.when(me_s != s)
        def _():
            remote(stsend.at[s], stin.at[s], xsem.at[0, s], xsem.at[1, s], (s, me_z)).wait_recv()
    for s in range(seqs):
        landed_from(0, s)
        piece_in = rows_in[0, s].astype(F32)
        rows_out[:, s * inner : s * inner + in1] = piece_in[:, :in1]
    for d in range(1, seqs):
        head_along(d).wait_recv()
    map_sums = [jnp.zeros((block, STATE), F32), jnp.zeros((block, STATE), F32)]
    for s in range(seqs):
        landed_from(1, s)
        piece_in = rows_in[1, s].astype(F32)
        rows_out[:, s * inner + in1 : (s + 1) * inner] = piece_in[:, :in2]
        base = full + 2 * STATE + s * hp
        rows_out[:, base : base + hp] = stin[s, :, :hp].astype(F32)
        map_sums[s % 2] = map_sums[s % 2] + piece_in[:, w2 : w2 + STATE]
    rows_out[:, full : full + 2 * STATE] = jnp.concatenate(map_sums, axis=1)
    sums = hall[0]
    for s in range(1, seqs):
        sums = sums + hall[s]
    head_out[...] = sums[:3, :heads]

    for g in (0, 1):
        for p in (0, 1):
            for way in (0, 1):
                for t in range(zeros):
                    ahead = me_z < t if way == 0 else me_z > t

                    @pl.when(ahead)
                    def _():
                        back_flow(g, way, t, p).wait_send()
    for d in range(1, zeros):
        steps_copy(d).wait_send()
        head_copy(d).wait_send()
    for d in range(1, seqs):
        head_along(d).wait_send()
    for s in range(seqs):
        @pl.when(me_s != s)
        def _():
            along(0, s).wait_send()
            along(1, s).wait_send()
            steps_along(s).wait_send()
    for i in range(chips):
        @pl.when(i != chip)
        def _():
            token_send(i).wait_send()


def mixer_backward(hidden, cotangent, weight, bias, log, gain, seqs, zeros, hp):
    length, model = hidden.shape
    rows = weight.shape[0]
    heads = bias.shape[1]
    inner = hp * HEAD_DIM
    slots = up(hp, 8)
    (n1, w1), (n2, w2) = groups_of(hp)
    wide = 2 * STATE + w1 + w2
    ends = max(w1, w2 + STATE)
    block = rows // seqs
    chips = seqs // 2
    total = seqs * length
    full = seqs * inner
    span = up(inner + (HEAD_DIM if hp % 2 else 0), 128)
    lanes = up(heads, 128)
    dma = pltpu.SemaphoreType.DMA
    vmem = pl.BlockSpec(memory_space=pltpu.VMEM)
    anywhere = pl.BlockSpec(memory_space=pl.ANY)
    return pl.pallas_call(
        functools.partial(mixer_backward_kernel, seqs, zeros, hp),
        out_shape=(
            jax.ShapeDtypeStruct((length, model), BF16),
            jax.ShapeDtypeStruct((block, full + 2 * STATE + heads), F32),
            jax.ShapeDtypeStruct((3, heads), F32),
        ),
        in_specs=[anywhere] * 3 + [vmem] * 3,
        out_specs=(vmem,) * 3,
        scratch_shapes=[
            pltpu.VMEM((rows, span), BF16),
            pltpu.VMEM((rows, heads), BF16),
            pltpu.VMEM((length, full), BF16),
            pltpu.VMEM((full, length), BF16),
            pltpu.VMEM((seqs, length, model), BF16),
            pltpu.VMEM((model, total), BF16),
            pltpu.VMEM((model, wide), BF16),
            pltpu.VMEM((zeros, 2 * STATE + w1, rows), BF16),
            pltpu.VMEM((wide, total), F32),
            pltpu.VMEM((seqs, inner, length), BF16),
            pltpu.VMEM((seqs, inner, length), F32),
            pltpu.VMEM((seqs, inner, length), BF16),
            pltpu.VMEM((seqs + 1, inner, STATE), BF16),
            pltpu.VMEM((wide + STATE, total), BF16),
            pltpu.VMEM((inner, STATE), F32),
            pltpu.VMEM((3, slots, length), F32),
            pltpu.VMEM((seqs * slots, length), F32),
            pltpu.VMEM((seqs * slots, length), F32),
            pltpu.VMEM((seqs, length, length), F32),
            pltpu.VMEM((seqs * slots, length), F32),
            pltpu.VMEM((2, seqs, STATE, length), F32),
            pltpu.VMEM((seqs, STATE, length), F32),
            pltpu.VMEM((chips, 2, model, length), F32),
            pltpu.VMEM((chips, model, length), F32),
            pltpu.VMEM((chips, model, length), BF16),
            pltpu.VMEM((chips, model, length), BF16),
            pltpu.VMEM((2, zeros, 2, seqs // 2, block, ends), BF16),
            pltpu.VMEM((2, zeros, 2, seqs // 2, block, ends), BF16),
            pltpu.VMEM((2, zeros, 2, seqs // 2, block, ends), BF16),
            pltpu.VMEM((2, seqs, block, ends), BF16),
            pltpu.VMEM((2, seqs, block, ends), BF16),
            pltpu.VMEM((zeros, 8, lanes), F32),
            pltpu.VMEM((8, lanes), F32),
            pltpu.VMEM((8, lanes), F32),
            pltpu.VMEM((seqs, 8, lanes), F32),
            pltpu.VMEM((seqs, STATE, length), BF16),
            pltpu.VMEM((seqs, STATE, length), BF16),
            pltpu.VMEM((seqs, length, length), F32),
            pltpu.VMEM((zeros, block, seqs * 16), BF16),
            pltpu.VMEM((zeros, block, seqs * 16), BF16),
            pltpu.VMEM((seqs, block, 16), BF16),
            pltpu.VMEM((seqs, block, 16), BF16),
            dma((2, 2, 2, zeros + 1, 2)),
            dma((2, seqs)),
            dma((2, seqs)),
            dma((2, seqs)),
            dma((2, zeros)),
            dma((2, seqs)),
            dma((2, chips, 2)),
            dma((2, chips)),
            dma((2, 2, 2, zeros, 2)),
            dma((2, seqs)),
            dma((2, zeros)),
            dma((2, 2, seqs)),
            dma((5,)),
            dma((2, zeros)),
            dma((2, seqs)),
        ],
        compiler_params=pltpu.CompilerParams(
            collective_id=0, has_side_effects=True, vmem_limit_bytes=63 * 1024 * 1024
        ),
        name="mixer_backward",
    )(hidden, cotangent, weight, bias, log, gain)


def store_kernel(*refs):
    count = len(refs) // 2
    sem = refs[-1]
    copies = [pltpu.make_async_copy(refs[i], refs[count + i], sem.at[i]) for i in range(count)]
    for copy in copies:
        copy.start()
    for copy in copies:
        copy.wait()


def store(*arrays):
    return pl.pallas_call(
        store_kernel,
        out_shape=tuple(jax.ShapeDtypeStruct(a.shape, a.dtype) for a in arrays),
        in_specs=[pl.BlockSpec(memory_space=pltpu.VMEM)] * len(arrays),
        out_specs=(pl.BlockSpec(memory_space=pl.ANY),) * len(arrays),
        scratch_shapes=[pltpu.SemaphoreType.DMA((len(arrays),))],
        name="store",
    )(*arrays)


def body(seqs, zeros, hidden, output_grad, input_weight, step_bias, decay_log, skip_gain):
    heads = step_bias.shape[0]
    hp = up(heads, seqs) // seqs
    spare = seqs * hp - heads
    full, total = heads * HEAD_DIM, seqs * hp * HEAD_DIM
    tokens, cot, weight = hidden[0], output_grad[0], input_weight
    params = [step_bias, decay_log, skip_gain]
    if spare:
        cot = jnp.pad(cot, ((0, 0), (0, total - full)))
        gap = jnp.zeros((weight.shape[0], total - full), BF16)
        few = jnp.zeros((weight.shape[0], spare), BF16)
        weight = jnp.concatenate([weight[:, :full], gap, weight[:, full:], few], axis=1)
        params = [jnp.pad(v, (0, spare)) for v in params]
    token_grad, weight_grad, head_grads = mixer_backward(
        tokens, cot, weight, *[v[None] for v in params], seqs, zeros, hp
    )
    token_grad, weight_grad, head_grads = store(token_grad, weight_grad, head_grads)
    if spare:
        weight_grad = jnp.concatenate(
            [weight_grad[:, :full], weight_grad[:, total : total + 2 * STATE + heads]], axis=1
        )
        head_grads = head_grads[:, :heads]
    return (token_grad[None], weight_grad, head_grads)


def solution(mesh):
    placed = (P("zero", "seq", None), P("zero", "seq", None), P("zero", None), P(), P(), P())
    return jax.shard_map(
        functools.partial(body, mesh.shape["seq"], mesh.shape["zero"]),
        mesh=mesh,
        in_specs=placed,
        out_specs=(P("zero", "seq", None), P(("seq", "zero"), None), P()),
        check_vma=False,
    )
```

time: 82.4 us -> 75.6 us (0.917)
  local copies, waits for them, and re-layouts: 4.78 us -> 0 us
  Pallas kernels: 76.7 us -> 73.9 us
    pallas_call x1, Pallas kernels: 76.7 us -> 71.9 us  [mixer_backward(): pl.pallas_call(functools.partial(mixer_backward_kernel, seqs, zeros, hp),...]
    unnamed x3 -> x0, local copies, waits for them, and re-layouts: 4.78 us -> none
    pallas_call x0 -> x1, Pallas kernels: none -> 2.02 us  [store(): pl.pallas_call(store_kernel, out_shape=tuple((jax.ShapeDtypeStruct(a.shap...]
where the time goes in v2:
time: 75.6 us; the launch traced here: 74.6 us
  Pallas kernels  73.9 us (98%)
    pallas_call x1, Pallas kernels, mixer_backward(): pl.pallas_call(functools.partial(mixer_backward_kernel, seqs, zeros, hp),...  71.9 us
    pallas_call x1, Pallas kernels, store(): pl.pallas_call(store_kernel, out_shape=tuple((jax.ShapeDtypeStruct(a.shap...  2.02 us

profile of v2, /device:TPU:0, one launch (start us, length us, event | category | flops | bytes accessed | tf_op | source)
XLA Modules:
  0.0 74.6 jit_solution(16649930667292907121)
XLA Ops:
  0.6 71.9 %mixer_backward.1 = (bf16[128,1280]{1,0:T(8,128)(2,1)}, f32[40,2856]{1,0:T(8,128)}, f32[3,40]{1,0:T(4,128)}) custom-call(bf16[128,1280]{1,0:T(8,128)(2,1)} %bitcast.7, bf16[128,2560]{1,0:T(8,128)(2,1)} %bitcast.6, bf16[320,2856]{1,0:T(8,128)(2,1)} %weight.1, f32[1,40]{1,0:T(1,128)} %bitcast.8, f32[1,40]{1,0:T(1,128)} %bitcast.9, f32[1,40]{1,0:T(1,128)} %bitcast.10), custom_call_target="tpu_custom_call" | custom-call | tf_op jit(solution)/shard_map/mixer_backward/pallas_call | solution.py:902
  72.5 2.0 %store.1 = (bf16[128,1280]{1,0:T(8,128)(2,1)}, f32[40,2856]{1,0:T(8,128)}, f32[3,40]{1,0:T(4,128)}) custom-call(bf16[128,1280]{1,0:T(8,128)(2,1)} %get-tuple-element.9.refs_0_, f32[40,2856]{1,0:T(8,128)} %get-tuple-element.10.refs_1_, f32[3,40]{1,0:T(4,128)} %get-tuple-element.11.refs_2_), custom_call_target="tpu_custom_call" | custom-call | tf_op jit(solution)/shard_map/store/pallas_call | solution.py:988

commit v3 on v2

--- a/solution.py
+++ b/solution.py
@@ -48,12 +48,12 @@
 def mixer_backward_kernel(
     seqs, zeros, hp,
     hidden, cotangent, weight, bias_in, log_in, gain_in,
-    hid, rows_out, head_out,
-    window, tiny, cotv, cott,
+    hid_hbm, rows_hbm, head_hbm,
+    hid, rows_out, head_out, window, tiny, cotv, cott,
     toks, tokt, wall, wallt, pre, dys, xs, tails, states, grads, grad, acc, steps, cums, cumt, sigr,
-    maps, got_map, part, got_part, sent, tok_in, wbuf, rflow, lflow, zsend, rows_in, hin, hsum, hmine, hall,
+    maps, got_map, wall2, mgrads, sgrads, sent, tok_in, wbuf, rflow, lflow, zsend, rows_in, hin, hsum, hmine, hall,
     ins, outs, scores, swbuf, swin, stsend, stin,
-    asem, tsem, psem, csem, ssem, msem, dsem, ksem, rsem, gsem, hsem, wsem, loc, ysem, xsem,
+    asem, tsem, psem, csem, ssem, msem, dsem, ksem, rsem, gsem, hsem, wsem, loc, ysem, xsem, qsem,
 ):
     me_s, me_z = lax.axis_index("seq"), lax.axis_index("zero")
     chips = seqs // 2
@@ -134,7 +134,7 @@
         at = me_z - h if way == 0 else me_z + h
         return remote(
             piece(g, at, p), piece(g, at, p),
-            asem.at[g, way, 0, h, p], asem.at[g, way, 1, h + (1 - recv), p],
+            asem.at[g, way, 0, min(h, last_z - 1), p], asem.at[g, way, 1, h - recv, p],
             up_peer if way == 0 else down_peer,
         )
 
@@ -320,9 +320,12 @@
     cots = []
     for d in range(1, seqs):
         peer = lax.rem(me_s + d, seqs)
-        cots.append(remote(cot_of(peer), dys.at[me_s], csem.at[0, d], csem.at[1, d], (peer, me_z)))
+        cots.append(remote(cot_of(peer), dys.at[me_s], csem.at[0], csem.at[1], (peer, me_z)))
     for copy in cots:
         copy.start()
+    all_cots = remote(
+        dys.at[pl.ds(0, seqs - 1)], dys.at[pl.ds(0, seqs - 1)], csem.at[0], csem.at[1], sibling
+    )
     if not square:
         rest = to_sibling + rest
     for copy in rest:
@@ -504,6 +507,10 @@
             grads[pl.ds(out_at, STATE), at] = d_out.astype(BF16)
             map_copy(k).start()
 
+            @pl.when(lax.rem(k, 2) != core)
+            def _():
+                swap(k // 2, k).start()
+
     def both_ways(g):
         def ahead(k, carry):
             forward(g, k)
@@ -514,20 +521,19 @@
             return carry
 
         here = slice(0, in1) if g == 0 else slice(in1, inner)
-        lax.fori_loop(0, chunks, ahead, 0)
+        lax.fori_loop(0, chunks, ahead, 0, unroll=2)
         states[chunks, here] = grad[here].astype(BF16)
         grad[here] = jnp.zeros_like(grad[here])
         if g == 0:
             for h in range(2, last_z):
                 late_hop(h, True)
-            for copy in cots:
-                copy.wait_recv()
+            all_cots.wait_recv()
         if g == 0:
-            lax.fori_loop(0, chunks, back, 0)
+            lax.fori_loop(0, chunks, back, 0, unroll=2)
         else:
-            lax.fori_loop(0, chunks // 2, back, 0)
+            lax.fori_loop(0, chunks // 2, back, 0, unroll=2)
             serve(0, 1)
-            lax.fori_loop(chunks // 2, chunks, back, 0)
+            lax.fori_loop(chunks // 2, chunks, back, 0, unroll=2)
 
     block = wbuf.shape[4]
     many = 4 if seqs % 4 == 0 else 2
@@ -554,7 +560,7 @@
         peer = up_peer if way == 0 else down_peer
         return remote(
             wbuf.at[g, t, p, :, :, pl.ds(0, sizes[g])], landed.at[g, t, p, :, :, pl.ds(0, sizes[g])],
-            rsem.at[g, way, 0, t, p], rsem.at[g, way, 1, t, p], peer,
+            rsem.at[g, way, 0, t - 1 + way, p], rsem.at[g, way, 1, t - 1 + way, p], peer,
         )
 
     def from_ends(g):
@@ -571,27 +577,17 @@
     def turn_of(n):
         return lax.rem(chip + 1 + n, chips)
 
-    def give(i, j):
-        at = pl.ds(j * low, low)
+    def swap(i, k):
         return remote(
-            part.at[i, 1 - core, at], got_part.at[i, at], dsem.at[0, i, j], dsem.at[1, i, j], sibling
+            grads.at[pl.ds(0, wide), pl.ds(pl.multiple_of(k * group, group), group)],
+            sgrads.at[:, pl.ds(pl.multiple_of(i * group, group), group)],
+            dsem.at[0, i], dsem.at[1, i], sibling,
         )
 
     def token_send(i):
         return remote(
             sent.at[i], tok_in.at[chip], ksem.at[0, i], ksem.at[1, chip], (i * 2 + core, me_z)
         )
-
-    def settle(n):
-        i = turn_of(n)
-        for j in (0, 1):
-            at = slice(j * low, (j + 1) * low)
-            give(i, j).wait_recv()
-            sent[i, at, :] = (part[i, core, at, :] + got_part[i, at, :]).astype(BF16)
-
-        @pl.when(i != chip)
-        def _():
-            token_send(i).start()
 
     def events(z):
         found = []
@@ -645,17 +641,25 @@
 
     def head_copy(d):
         return remote(
-            hmine, hin.at[me_z], hsem.at[0, d], hsem.at[1, d], (me_s, lax.rem(me_z + d, zeros))
+            hmine, hin.at[me_z], hsem.at[0], hsem.at[1], (me_s, lax.rem(me_z + d, zeros))
         )
 
     def head_along(d):
         return remote(
-            hsum, hall.at[me_s], gsem.at[0, d], gsem.at[1, d], (lax.rem(me_s + d, seqs), me_z)
-        )
+            hsum, hall.at[me_s], gsem.at[0], gsem.at[1], (lax.rem(me_s + d, seqs), me_z)
+        )
+
+    def all_heads():
+        few = pl.ds(0, zeros - 1)
+        return remote(hin.at[few], hin.at[few], hsem.at[0], hsem.at[1], sibling)
+
+    def all_steps():
+        few = pl.ds(0, zeros - 1)
+        return remote(swbuf.at[few], swin.at[few], ysem.at[0], ysem.at[1], sibling)
 
     def close_heads():
-        for d in range(1, zeros):
-            head_copy(d).wait_recv()
+        if zeros > 1:
+            all_heads().wait_recv()
         sums = hin[0]
         for d in range(1, zeros):
             sums = sums + hin[d]
@@ -674,7 +678,7 @@
                             flow(g, way, h, p, 0).wait_send()
         for j in range(zeros):
             shared(j).wait_send()
-        for copy in direct + to_sibling + cots:
+        for copy in direct + to_sibling + [all_cots]:
             copy.wait_send()
 
         def gone(k, carry):
@@ -683,8 +687,20 @@
 
         lax.fori_loop(0, chunks, gone, 0)
         for i in range(chips):
-            for j in (0, 1):
-                give(i, j).wait_send()
+            swap(i, 2 * i + 1 - core).wait_send()
+        columns_copy.wait_send()
+
+    def send_steps():
+        steps_grad = nt(tokt[...], grads[top : top + 16, :])
+        for t in range(zeros):
+            lines = [
+                steps_grad[(s * zeros + t) * block : (s * zeros + t + 1) * block] for s in range(seqs)
+            ]
+            swbuf[t] = jnp.concatenate(lines, axis=1).astype(BF16)
+        swin[me_z] = swbuf[me_z]
+
+        for d in range(1, zeros):
+            steps_copy(d).start()
 
     def finish_piece(z, g, p):
         if z > 0:
@@ -692,8 +708,8 @@
         if z < last_z:
             back_flow(g, 1, z, p).wait_recv()
         if g == 1 and p == 0:
-            for d in range(1, zeros):
-                steps_copy(d).wait_recv()
+            if zeros > 1:
+                all_steps().wait_recv()
             total = swin[0].astype(F32)
             for d in range(1, zeros):
                 total = total + swin[d].astype(F32)
@@ -721,16 +737,16 @@
         lanes = pl.ds(0, sizes[g])
         return remote(
             zsend.at[g, s, :, lanes], rows_in.at[g, me_s, :, lanes],
-            wsem.at[g, 0, s], wsem.at[g, 1, me_s], (s, me_z),
+            wsem.at[g, 0], wsem.at[g, 1], (s, me_z),
         )
 
     def steps_along(s):
-        return remote(stsend.at[s], stin.at[me_s], xsem.at[0, s], xsem.at[1, me_s], (s, me_z))
+        return remote(stsend.at[s], stin.at[me_s], xsem.at[0], xsem.at[1], (s, me_z))
 
     def steps_copy(d):
         target = lax.rem(me_z + d, zeros)
         return remote(
-            swbuf.at[target], swin.at[me_z], ysem.at[0, d], ysem.at[1, d], (me_s, target)
+            swbuf.at[target], swin.at[me_z], ysem.at[0], ysem.at[1], (me_s, target)
         )
 
     grad[...] = jnp.zeros_like(grad)
@@ -745,6 +761,13 @@
     for h in range(1, zeros):
         late_hop(h, False)
 
+    columns_copy = remote(
+        wall.at[:, pl.ds(v1, wide - v1)], wall2.at[:, pl.ds(v1, wide - v1)], qsem.at[0], qsem.at[1], sibling
+    )
+    columns_copy.start()
+    wall2[:, 0:STATE] = wall[:, STATE:v1]
+    wall2[:, STATE:v1] = wall[:, 0:STATE]
+
     def project_late(i, carry):
         cols = pl.ds(pl.multiple_of(i * batch, batch), batch)
         pre[v2:wide, cols] = tn(wall[:, v2:wide], tokt[:, cols])
@@ -754,14 +777,29 @@
     both_ways(1)
     serve(1, 2)
 
-    for j in (0, 1):
-        at = slice(j * low, (j + 1) * low)
-        product = nn(wall[at, :], grads[0:wide, :])
-        for k in range(chunks):
-            part[k // 2, k % 2, at, :] = product[:, k * group : (k + 1) * group]
-        for n in range(chips):
-            give(turn_of(n), j).start()
-        serve(2 + j, 3 + j)
+    send_steps()
+    for i in range(chips):
+        at = pl.ds(pl.multiple_of((2 * i + core) * group, group), group)
+        mgrads[:, i * group : (i + 1) * group] = grads[0:wide, at]
+    columns_copy.wait_recv()
+    for i in range(chips):
+        swap(i, 2 * i + core).wait_recv()
+    def back_project(j, carry):
+        at = pl.ds(pl.multiple_of(j * low, low), low)
+        product = nn(wall[at, :], mgrads[...]) + nn(wall2[at, :], sgrads[...])
+        for i in range(chips):
+            sent[i, at, :] = product[:, i * group : (i + 1) * group].astype(BF16)
+        for turn_j in (0, 1):
+            @pl.when(j == turn_j)
+            def _():
+                serve(2 + turn_j, 3 + turn_j)
+        return carry
+
+    lax.fori_loop(0, 2, back_project, 0)
+    for n in range(chips):
+        @pl.when(turn_of(n) != chip)
+        def _():
+            token_send(turn_of(n)).start()
 
     def merge(k, carry):
         map_copy(k).wait_recv()
@@ -790,19 +828,6 @@
     weigh(1, v2, w2 + STATE)
     from_ends(1)
 
-    steps_grad = nt(tokt[...], grads[top : top + 16, :])
-    for t in range(zeros):
-        lines = [
-            steps_grad[(s * zeros + t) * block : (s * zeros + t + 1) * block] for s in range(seqs)
-        ]
-        swbuf[t] = jnp.concatenate(lines, axis=1).astype(BF16)
-    swin[me_z] = swbuf[me_z]
-
-    for d in range(1, zeros):
-        steps_copy(d).start()
-
-    for n in range(chips):
-        settle(n)
     serve(None, None)
 
     for g in (0, 1):
@@ -821,64 +846,69 @@
             value = value + tok_in[source, at, :].astype(F32)
         hid[:, at] = value.T.astype(BF16)
 
-    def landed_from(g, s):
-        @pl.when(me_s != s)
-        def _():
-            lanes = pl.ds(0, sizes[g])
-            remote(
-                zsend.at[g, s, :, lanes], rows_in.at[g, s, :, lanes],
-                wsem.at[g, 0, s], wsem.at[g, 1, s], (s, me_z),
-            ).wait_recv()
-
-    stin[me_s] = stsend[me_s]
+    leaving = [pltpu.make_async_copy(hid, hid_hbm, loc.at[0])]
+    leaving[0].start()
+
+    def whole(src, dst, sems, count):
+        few = pl.ds(0, count)
+        return remote(src.at[few], dst.at[few], sems.at[0], sems.at[1], sibling)
+
+    def along_whole(g):
+        lanes = pl.ds(0, sizes[g])
+        few = pl.ds(0, seqs - 1)
+        return remote(
+            zsend.at[g, few, :, lanes], rows_in.at[g, few, :, lanes], wsem.at[g, 0], wsem.at[g, 1], sibling
+        )
+
+    along_whole(0).wait_recv()
     for s in range(seqs):
-        @pl.when(me_s != s)
-        def _():
-            remote(stsend.at[s], stin.at[s], xsem.at[0, s], xsem.at[1, s], (s, me_z)).wait_recv()
-    for s in range(seqs):
-        landed_from(0, s)
         piece_in = rows_in[0, s].astype(F32)
         rows_out[:, s * inner : s * inner + in1] = piece_in[:, :in1]
-    for d in range(1, seqs):
-        head_along(d).wait_recv()
+    whole(hall, hall, gsem, seqs - 1).wait_recv()
+    sums = hall[0]
+    for s in range(1, seqs):
+        sums = sums + hall[s]
+    head_out[...] = sums[:3, :heads]
+    leaving.append(pltpu.make_async_copy(head_out, head_hbm, loc.at[1]))
+    leaving[1].start()
     map_sums = [jnp.zeros((block, STATE), F32), jnp.zeros((block, STATE), F32)]
+    stin[me_s] = stsend[me_s]
+    whole(stsend, stin, xsem, seqs - 1).wait_recv()
+    along_whole(1).wait_recv()
     for s in range(seqs):
-        landed_from(1, s)
         piece_in = rows_in[1, s].astype(F32)
         rows_out[:, s * inner + in1 : (s + 1) * inner] = piece_in[:, :in2]
         base = full + 2 * STATE + s * hp
         rows_out[:, base : base + hp] = stin[s, :, :hp].astype(F32)
         map_sums[s % 2] = map_sums[s % 2] + piece_in[:, w2 : w2 + STATE]
     rows_out[:, full : full + 2 * STATE] = jnp.concatenate(map_sums, axis=1)
-    sums = hall[0]
-    for s in range(1, seqs):
-        sums = sums + hall[s]
-    head_out[...] = sums[:3, :heads]
+    leaving.append(pltpu.make_async_copy(rows_out, rows_hbm, loc.at[2]))
+    leaving[2].start()
 
     for g in (0, 1):
         for p in (0, 1):
             for way in (0, 1):
                 for t in range(zeros):
+                    if t == (0 if way == 0 else last_z):
+                        continue
                     ahead = me_z < t if way == 0 else me_z > t
 
                     @pl.when(ahead)
                     def _():
                         back_flow(g, way, t, p).wait_send()
-    for d in range(1, zeros):
-        steps_copy(d).wait_send()
-        head_copy(d).wait_send()
-    for d in range(1, seqs):
-        head_along(d).wait_send()
-    for s in range(seqs):
-        @pl.when(me_s != s)
-        def _():
-            along(0, s).wait_send()
-            along(1, s).wait_send()
-            steps_along(s).wait_send()
+    if zeros > 1:
+        all_steps().wait_send()
+        all_heads().wait_send()
+    whole(hall, hall, gsem, seqs - 1).wait_send()
+    along_whole(0).wait_send()
+    along_whole(1).wait_send()
+    whole(stsend, stin, xsem, seqs - 1).wait_send()
     for i in range(chips):
         @pl.when(i != chip)
         def _():
             token_send(i).wait_send()
+    for copy in leaving:
+        copy.wait()
 
 
 def mixer_backward(hidden, cotangent, weight, bias, log, gain, seqs, zeros, hp):
@@ -892,6 +922,7 @@
     ends = max(w1, w2 + STATE)
     block = rows // seqs
     chips = seqs // 2
+    last = max(zeros - 1, 1)
     total = seqs * length
     full = seqs * inner
     span = up(inner + (HEAD_DIM if hp % 2 else 0), 128)
@@ -907,8 +938,11 @@
             jax.ShapeDtypeStruct((3, heads), F32),
         ),
         in_specs=[anywhere] * 3 + [vmem] * 3,
-        out_specs=(vmem,) * 3,
+        out_specs=(anywhere,) * 3,
         scratch_shapes=[
+            pltpu.VMEM((length, model), BF16),
+            pltpu.VMEM((block, full + 2 * STATE + heads), F32),
+            pltpu.VMEM((3, heads), F32),
             pltpu.VMEM((rows, span), BF16),
             pltpu.VMEM((rows, heads), BF16),
             pltpu.VMEM((length, full), BF16),
@@ -931,8 +965,9 @@
             pltpu.VMEM((seqs * slots, length), F32),
             pltpu.VMEM((2, seqs, STATE, length), F32),
             pltpu.VMEM((seqs, STATE, length), F32),
-            pltpu.VMEM((chips, 2, model, length), F32),
-            pltpu.VMEM((chips, model, length), F32),
+            pltpu.VMEM((model, wide), BF16),
+            pltpu.VMEM((wide, chips * length), BF16),
+            pltpu.VMEM((wide, chips * length), BF16),
             pltpu.VMEM((chips, model, length), BF16),
             pltpu.VMEM((chips, model, length), BF16),
             pltpu.VMEM((2, zeros, 2, seqs // 2, block, ends), BF16),
@@ -951,21 +986,22 @@
             pltpu.VMEM((zeros, block, seqs * 16), BF16),
             pltpu.VMEM((seqs, block, 16), BF16),
             pltpu.VMEM((seqs, block, 16), BF16),
-            dma((2, 2, 2, zeros + 1, 2)),
-            dma((2, seqs)),
-            dma((2, seqs)),
-            dma((2, seqs)),
+            dma((2, 2, 2, last, 2)),
+            dma((2, max(4, chips))),
+            dma((2, chips)),
+            dma((2,)),
             dma((2, zeros)),
             dma((2, seqs)),
-            dma((2, chips, 2)),
             dma((2, chips)),
-            dma((2, 2, 2, zeros, 2)),
-            dma((2, seqs)),
-            dma((2, zeros)),
-            dma((2, 2, seqs)),
+            dma((2, chips)),
+            dma((2, 2, 2, last, 2)),
+            dma((2,)),
+            dma((2,)),
+            dma((2, 2)),
             dma((5,)),
-            dma((2, zeros)),
-            dma((2, seqs)),
+            dma((2,)),
+            dma((2,)),
+            dma((2,)),
         ],
         compiler_params=pltpu.CompilerParams(
             collective_id=0, has_side_effects=True, vmem_limit_bytes=63 * 1024 * 1024
@@ -975,12 +1011,18 @@
 
 
 def store_kernel(*refs):
-    count = len(refs) // 2
+    count = len(refs) // 3
     sem = refs[-1]
-    copies = [pltpu.make_async_copy(refs[i], refs[count + i], sem.at[i]) for i in range(count)]
-    for copy in copies:
+    takes = [pltpu.make_async_copy(refs[i], refs[2 * count + i], sem.at[0, i]) for i in range(count)]
+    puts = [
+        pltpu.make_async_copy(refs[2 * count + i], refs[count + i], sem.at[1, i]) for i in range(count)
+    ]
+    for copy in takes:
         copy.start()
-    for copy in copies:
+    for take, put in zip(takes, puts):
+        take.wait()
+        put.start()
+    for copy in puts:
         copy.wait()
 
 
@@ -988,9 +1030,10 @@
     return pl.pallas_call(
         store_kernel,
         out_shape=tuple(jax.ShapeDtypeStruct(a.shape, a.dtype) for a in arrays),
-        in_specs=[pl.BlockSpec(memory_space=pltpu.VMEM)] * len(arrays),
+        in_specs=[pl.BlockSpec(memory_space=pl.ANY)] * len(arrays),
         out_specs=(pl.BlockSpec(memory_space=pl.ANY),) * len(arrays),
-        scratch_shapes=[pltpu.SemaphoreType.DMA((len(arrays),))],
+        scratch_shapes=[pltpu.VMEM(a.shape, a.dtype) for a in arrays]
+        + [pltpu.SemaphoreType.DMA((2, len(arrays)))],
         name="store",
     )(*arrays)
 

time: 75.6 us -> 71.2 us (0.942)
  Pallas kernels: 73.9 us -> 69.8 us
    pallas_call x1, Pallas kernels: 71.9 us -> 67.9 us  [mixer_backward(): pl.pallas_call(functools.partial(mixer_backward_kernel, seqs, zeros, hp),...]
where the time goes in v3:
time: 71.2 us; the launch traced here: 70.5 us
  Pallas kernels  69.8 us (98%)
    pallas_call x1, Pallas kernels, mixer_backward(): pl.pallas_call(functools.partial(mixer_backward_kernel, seqs, zeros, hp),...  67.9 us
    pallas_call x1, Pallas kernels, store(): pl.pallas_call(store_kernel, out_shape=tuple((jax.ShapeDtypeStruct(a.shap...  1.95 us

profile of v3, /device:TPU:0, one launch (start us, length us, event | category | flops | bytes accessed | tf_op | source)
XLA Modules:
  0.0 70.5 jit_solution(6449120335418874083)
XLA Ops:
  0.6 67.9 %mixer_backward.1 = (bf16[128,1280]{1,0:T(8,128)(2,1)}, f32[40,2856]{1,0:T(8,128)}, f32[3,40]{1,0:T(4,128)}) custom-call(bf16[128,1280]{1,0:T(8,128)(2,1)} %bitcast.7, bf16[128,2560]{1,0:T(8,128)(2,1)} %bitcast.6, bf16[320,2856]{1,0:T(8,128)(2,1)} %weight.1, f32[1,40]{1,0:T(1,128)} %bitcast.8, f32[1,40]{1,0:T(1,128)} %bitcast.9, f32[1,40]{1,0:T(1,128)} %bitcast.10), custom_call_target="tpu_custom_call" | custom-call | tf_op jit(solution)/shard_map/mixer_backward/pallas_call | solution.py:933
  68.5 1.9 %store.1 = (bf16[128,1280]{1,0:T(8,128)(2,1)}, f32[40,2856]{1,0:T(8,128)}, f32[3,40]{1,0:T(4,128)}) custom-call(bf16[128,1280]{1,0:T(8,128)(2,1)} %get-tuple-element.9.refs_0_, f32[40,2856]{1,0:T(8,128)} %get-tuple-element.10.refs_1_, f32[3,40]{1,0:T(4,128)} %get-tuple-element.11.refs_2_), custom_call_target="tpu_custom_call" | custom-call | tf_op jit(solution)/shard_map/store/pallas_call | solution.py:1030

commit v4 on v3

--- a/solution.py
+++ b/solution.py
@@ -51,7 +51,7 @@
     hid_hbm, rows_hbm, head_hbm,
     hid, rows_out, head_out, window, tiny, cotv, cott,
     toks, tokt, wall, wallt, pre, dys, xs, tails, states, grads, grad, acc, steps, cums, cumt, sigr,
-    maps, got_map, wall2, mgrads, sgrads, sent, tok_in, wbuf, rflow, lflow, zsend, rows_in, hin, hsum, hmine, hall,
+    maps, got_map, wall2, mgrads, sgrads, relay, sent, tok_in, wbuf, rflow, lflow, zsend, rows_in, hin, hsum, hmine, hall,
     ins, outs, scores, swbuf, swin, stsend, stin,
     asem, tsem, psem, csem, ssem, msem, dsem, ksem, rsem, gsem, hsem, wsem, loc, ysem, xsem, qsem,
 ):
@@ -188,7 +188,19 @@
         around = [flat, tall]
     else:
         around = [lax.rem(chip + d, chips) for d in range(1, chips)]
-    direct = [token(me_s, c * 2 + core, 0, length, i) for i, c in enumerate(around)]
+    if square:
+        direct = [
+            token(me_s, flat * 2 + core, 0, cut, 0),
+            token(me_s, tall * 2 + core, cut, length - cut, 1),
+            token(me_s, flat * 2 + core, cut, length - cut, 4),
+            token(me_s, tall * 2 + core, 0, cut, 5),
+        ]
+        onward = [
+            token(flat * 2 + core, tall * 2 + core, 0, cut, 2),
+            token(tall * 2 + core, flat * 2 + core, cut, length - cut, 3),
+        ]
+    else:
+        direct = [token(me_s, c * 2 + core, 0, length, i) for i, c in enumerate(around)]
     for copy in direct + to_sibling:
         copy.start()
     shared(me_z).start()
@@ -209,8 +221,16 @@
 
     dys[me_s] = cot_of(me_s)[...]
 
+    def send_on():
+        if square:
+            for i in (0, 1):
+                direct[i].wait_recv()
+                onward[i].start()
+
     def step_hop(h):
         for p in (0, 1):
+            if h == 1 and p == 1 and zeros > 2:
+                send_on()
             for way in (0, 1):
                 @pl.when(comes(way, h))
                 def _():
@@ -243,6 +263,8 @@
 
     if zeros > 2:
         step_hop(1)
+    else:
+        send_on()
 
     def chip_of(n):
         if square:
@@ -257,13 +279,8 @@
 
     early = 3 if square else 0
     if square:
-        onward = [
-            token(flat * 2 + core, tall * 2 + core, 0, cut, 2),
-            token(tall * 2 + core, flat * 2 + core, cut, length - cut, 3),
-        ]
-        for i in (0, 1):
+        for i in (2, 3):
             direct[i].wait_recv()
-            onward[i].start()
         direct += onward
         more = [passed(flat * 2 + core, 1), passed(tall * 2 + core, 2)]
         for copy in more:
@@ -273,6 +290,15 @@
             copy.wait_recv()
         lax.fori_loop(0, early, turn, 0)
 
+    cots = []
+    for d in range(1, seqs):
+        peer = lax.rem(me_s + d, seqs)
+        cots.append(remote(cot_of(peer), dys.at[me_s], csem.at[0], csem.at[1], (peer, me_z)))
+    for copy in cots:
+        copy.start()
+    all_cots = remote(
+        dys.at[pl.ds(0, seqs - 1)], dys.at[pl.ds(0, seqs - 1)], csem.at[0], csem.at[1], sibling
+    )
     for h in range(2, last_z):
         step_hop(h)
 
@@ -289,6 +315,15 @@
 
         lax.fori_loop(first, final, part_of, 0)
 
+    def project_all(j):
+        def part_of(n, carry):
+            at = pl.ds(pl.multiple_of(j * rows, rows), rows)
+            cols = pl.ds(pl.multiple_of(n * 2 * pairs, 2 * pairs), 2 * pairs)
+            pre[:v2, cols] += nn(wallt[j], tokt[at, cols])
+            return carry
+
+        lax.fori_loop(0, chips // 2, part_of, 0)
+
     def near(first, final, fresh):
         def one(j, carry):
             distance = jnp.abs(j - me_z)
@@ -302,9 +337,6 @@
             return carry
 
         lax.fori_loop(0, zeros, one, 0)
-
-    if early:
-        near(0, early, True)
 
     if square:
         token(far * 2 + core, tall * 2 + core, 0, cut, 2).wait_recv()
@@ -317,15 +349,8 @@
             rest.append(passed(lax.rem(chip - d + chips, chips) * 2 + core, d))
     for copy in rest:
         copy.start()
-    cots = []
-    for d in range(1, seqs):
-        peer = lax.rem(me_s + d, seqs)
-        cots.append(remote(cot_of(peer), dys.at[me_s], csem.at[0], csem.at[1], (peer, me_z)))
-    for copy in cots:
-        copy.start()
-    all_cots = remote(
-        dys.at[pl.ds(0, seqs - 1)], dys.at[pl.ds(0, seqs - 1)], csem.at[0], csem.at[1], sibling
-    )
+    if early:
+        near(0, early, True)
     if not square:
         rest = to_sibling + rest
     for copy in rest:
@@ -345,7 +370,7 @@
         @pl.when(far_end)
         def _():
             flip(last_z - me_z)
-            project(last_z - me_z, 0, chips)
+            project_all(last_z - me_z)
 
     in_at = pl.multiple_of((1 - core) * STATE, 128)
     out_at = pl.multiple_of(core * STATE, 128)
@@ -589,8 +614,29 @@
             sent.at[i], tok_in.at[chip], ksem.at[0, i], ksem.at[1, chip], (i * 2 + core, me_z)
         )
 
+    def plane_copy(part_no):
+        to_flat = part_no % 2 == 0
+        peer = (flat if to_flat else tall) * 2 + core
+        first_half = part_no in (0, 2, 5)
+        at = pl.ds(0 if first_half else low, low)
+        if part_no < 2:
+            src, dst = sent.at[far, at], relay.at[part_no]
+        else:
+            src, dst = sent.at[flat if to_flat else tall, at], tok_in.at[chip, at]
+        return remote(src, dst, ksem.at[0, part_no], ksem.at[1, part_no], (peer, me_z))
+
+    def relay_on():
+        if square:
+            for part_no, target, lo in ((1, flat, low), (0, tall, 0)):
+                plane_copy(part_no).wait_recv()
+                at = slice(lo, lo + low)
+                sent[target, at, :] = (
+                    sent[target, at, :].astype(F32) + relay[part_no].astype(F32)
+                ).astype(BF16)
+                plane_copy(4 + (1 - part_no)).start()
+
     def events(z):
-        found = []
+        found = [(9.7, 2, "relay", 0)]
         for g in (0, 1):
             for p in (0, 1):
                 ends = 0.0
@@ -633,6 +679,8 @@
                     wbuf[g, t, p].astype(F32) + landed[g, t, p].astype(F32)
                 ).astype(BF16)
                 back_flow(g, way, t, p).start()
+            elif what == "relay":
+                relay_on()
             elif what == "heads":
                 close_heads()
                 drain()
@@ -796,10 +844,14 @@
         return carry
 
     lax.fori_loop(0, 2, back_project, 0)
-    for n in range(chips):
-        @pl.when(turn_of(n) != chip)
-        def _():
-            token_send(turn_of(n)).start()
+    if square:
+        for part_no in (0, 1, 2, 3):
+            plane_copy(part_no).start()
+    else:
+        for n in range(chips):
+            @pl.when(turn_of(n) != chip)
+            def _():
+                token_send(turn_of(n)).start()
 
     def merge(k, carry):
         map_copy(k).wait_recv()
@@ -832,17 +884,22 @@
 
     for g in (0, 1):
         rows_in[g, me_s] = zsend[g, me_s]
-    for d in range(1, chips):
-        at = lax.rem(chip + d, chips)
-        remote(
-            sent.at[at], tok_in.at[at], ksem.at[0, at], ksem.at[1, at], (at * 2 + core, me_z)
-        ).wait_recv()
-    tok_in[chip] = sent[chip]
+    if square:
+        for part_no in (2, 3, 4, 5):
+            plane_copy(part_no).wait_recv()
+        sources = [flat, tall]
+    else:
+        for d in range(1, chips):
+            at = lax.rem(chip + d, chips)
+            remote(
+                sent.at[at], tok_in.at[at], ksem.at[0, at], ksem.at[1, at], (at * 2 + core, me_z)
+            ).wait_recv()
+        sources = [lax.rem(chip + d, chips) for d in range(1, chips)]
 
     for j in (0, 1):
         at = slice(j * low, (j + 1) * low)
-        value = tok_in[0, at, :].astype(F32)
-        for source in range(1, chips):
+        value = sent[chip, at, :].astype(F32)
+        for source in sources:
             value = value + tok_in[source, at, :].astype(F32)
         hid[:, at] = value.T.astype(BF16)
 
@@ -903,10 +960,14 @@
     along_whole(0).wait_send()
     along_whole(1).wait_send()
     whole(stsend, stin, xsem, seqs - 1).wait_send()
-    for i in range(chips):
-        @pl.when(i != chip)
-        def _():
-            token_send(i).wait_send()
+    if square:
+        for part_no in range(6):
+            plane_copy(part_no).wait_send()
+    else:
+        for i in range(chips):
+            @pl.when(i != chip)
+            def _():
+                token_send(i).wait_send()
     for copy in leaving:
         copy.wait()
 
@@ -968,6 +1029,7 @@
             pltpu.VMEM((model, wide), BF16),
             pltpu.VMEM((wide, chips * length), BF16),
             pltpu.VMEM((wide, chips * length), BF16),
+            pltpu.VMEM((2, model // 2, length), BF16),
             pltpu.VMEM((chips, model, length), BF16),
             pltpu.VMEM((chips, model, length), BF16),
             pltpu.VMEM((2, zeros, 2, seqs // 2, block, ends), BF16),
@@ -987,13 +1049,13 @@
             pltpu.VMEM((seqs, block, 16), BF16),
             pltpu.VMEM((seqs, block, 16), BF16),
             dma((2, 2, 2, last, 2)),
-            dma((2, max(4, chips))),
+            dma((2, max(6, chips))),
             dma((2, chips)),
             dma((2,)),
             dma((2, zeros)),
             dma((2, seqs)),
             dma((2, chips)),
-            dma((2, chips)),
+            dma((2, max(6, chips))),
             dma((2, 2, 2, last, 2)),
             dma((2,)),
             dma((2,)),

time: 71.2 us -> 67 us (0.941)
  Pallas kernels: 69.8 us -> 66.2 us
    pallas_call x1, Pallas kernels: 67.9 us -> 64.2 us  [mixer_backward(): pl.pallas_call(functools.partial(mixer_backward_kernel, seqs, zeros, hp),...]
where the time goes in v4:
time: 67 us; the launch traced here: 66.8 us
  Pallas kernels  66.2 us (99%)
    pallas_call x1, Pallas kernels, mixer_backward(): pl.pallas_call(functools.partial(mixer_backward_kernel, seqs, zeros, hp),...  64.2 us
    pallas_call x1, Pallas kernels, store(): pl.pallas_call(store_kernel, out_shape=tuple((jax.ShapeDtypeStruct(a.shap...  1.95 us

profile of v4, /device:TPU:0, one launch (start us, length us, event | category | flops | bytes accessed | tf_op | source)
XLA Modules:
  0.0 66.8 jit_solution(1561813732426353782)
XLA Ops:
  0.6 64.2 %mixer_backward.1 = (bf16[128,1280]{1,0:T(8,128)(2,1)}, f32[40,2856]{1,0:T(8,128)}, f32[3,40]{1,0:T(4,128)}) custom-call(bf16[128,1280]{1,0:T(8,128)(2,1)} %bitcast.7, bf16[128,2560]{1,0:T(8,128)(2,1)} %bitcast.6, bf16[320,2856]{1,0:T(8,128)(2,1)} %weight.1, f32[1,40]{1,0:T(1,128)} %bitcast.8, f32[1,40]{1,0:T(1,128)} %bitcast.9, f32[1,40]{1,0:T(1,128)} %bitcast.10), custom_call_target="tpu_custom_call" | custom-call | tf_op jit(solution)/shard_map/mixer_backward/pallas_call | solution.py:994
  64.9 1.9 %store.1 = (bf16[128,1280]{1,0:T(8,128)(2,1)}, f32[40,2856]{1,0:T(8,128)}, f32[3,40]{1,0:T(4,128)}) custom-call(bf16[128,1280]{1,0:T(8,128)(2,1)} %get-tuple-element.9.refs_0_, f32[40,2856]{1,0:T(8,128)} %get-tuple-element.10.refs_1_, f32[3,40]{1,0:T(4,128)} %get-tuple-element.11.refs_2_), custom_call_target="tpu_custom_call" | custom-call | tf_op jit(solution)/shard_map/store/pallas_call | solution.py:1092

commit v5 on v4

--- a/solution.py
+++ b/solution.py
@@ -546,7 +546,7 @@
             return carry
 
         here = slice(0, in1) if g == 0 else slice(in1, inner)
-        lax.fori_loop(0, chunks, ahead, 0, unroll=2)
+        lax.fori_loop(0, chunks, ahead, 0, unroll=4)
         states[chunks, here] = grad[here].astype(BF16)
         grad[here] = jnp.zeros_like(grad[here])
         if g == 0:

time: 67 us -> 66.6 us (level)
  no operation moved by 1% of the time
where the time goes in v5:
time: 66.6 us; the launch traced here: 66.4 us
  Pallas kernels  65.7 us (99%)
    pallas_call x1, Pallas kernels, mixer_backward(): pl.pallas_call(functools.partial(mixer_backward_kernel, seqs, zeros, hp),...  63.8 us
    pallas_call x1, Pallas kernels, store(): pl.pallas_call(store_kernel, out_shape=tuple((jax.ShapeDtypeStruct(a.shap...  1.95 us

profile of v5, /device:TPU:0, one launch (start us, length us, event | category | flops | bytes accessed | tf_op | source)
XLA Modules:
  0.0 66.4 jit_solution(1293327165970013136)
XLA Ops:
  0.6 63.8 %mixer_backward.1 = (bf16[128,1280]{1,0:T(8,128)(2,1)}, f32[40,2856]{1,0:T(8,128)}, f32[3,40]{1,0:T(4,128)}) custom-call(bf16[128,1280]{1,0:T(8,128)(2,1)} %bitcast.7, bf16[128,2560]{1,0:T(8,128)(2,1)} %bitcast.6, bf16[320,2856]{1,0:T(8,128)(2,1)} %weight.1, f32[1,40]{1,0:T(1,128)} %bitcast.8, f32[1,40]{1,0:T(1,128)} %bitcast.9, f32[1,40]{1,0:T(1,128)} %bitcast.10), custom_call_target="tpu_custom_call" | custom-call | tf_op jit(solution)/shard_map/mixer_backward/pallas_call | solution.py:994
  64.4 1.9 %store.1 = (bf16[128,1280]{1,0:T(8,128)(2,1)}, f32[40,2856]{1,0:T(8,128)}, f32[3,40]{1,0:T(4,128)}) custom-call(bf16[128,1280]{1,0:T(8,128)(2,1)} %get-tuple-element.9.refs_0_, f32[40,2856]{1,0:T(8,128)} %get-tuple-element.10.refs_1_, f32[3,40]{1,0:T(4,128)} %get-tuple-element.11.refs_2_), custom_call_target="tpu_custom_call" | custom-call | tf_op jit(solution)/shard_map/store/pallas_call | solution.py:1092
